TPU v7x, 256 devices: a whole 4x4x8 slice. The times are simulated.
256 devices in a mesh: seq: 16 (over x, z_lo), row: 2 (over core), col: 8 (over z_hi, y).
Axes of the slice: x: 4, y: 4, z: 8 (z_hi: 2, z_lo: 4; z = z_hi * 4 + z_lo), core: 2. Of those that a mesh axis runs over, the one named last changes fastest.
Arguments:
- tokens: bfloat16 [8192, 6144], P('seq', ('row', 'col')), may hold values from -20 to 20
- ln_gain: bfloat16 [6144], P(('row', 'col')), may hold values from 0.099609375 to 1.8984375
- ln_bias: bfloat16 [6144], P(('row', 'col')), may hold values from -1.5 to 1.5
- w_qkv: bfloat16 [3, 6144, 4096], P(None, 'row', 'col'), may hold values from -3 to 3
- w_out: bfloat16 [4096, 6144], P('col', 'row'), may hold values from -0.5 to 0.5
Outputs:
- attended: bfloat16 [8192, 6144], P('seq', ('row', 'col'))
All inputs are finite; a program needn't handle non-finite values.
Results may differ from a plain program's by a relative error of at most 0.014.
Values may be sent and summed in bfloat16 or wider, within the bound.
No kernel may reach another device: no remote copies, remote signals or barrier semaphores. Data moves between devices by JAX's collectives and lax.ppermute only.
A program may use at most 128 MiB of HBM per device.

v0:
```python
import functools
import math

import jax
import jax.numpy as jnp
from jax import lax
from jax.experimental import pallas as pl
from jax.experimental.pallas import tpu as pltpu
from jax.sharding import Mesh
from jax.sharding import PartitionSpec as P

D = 6144
HD = 128
EPS = 0.25
F32 = jnp.float32
BF16 = jnp.bfloat16
SCORE_LOG2 = math.log2(math.e) / math.sqrt(HD)
SPLIT = 1
VMEM = pl.BlockSpec(memory_space=pltpu.VMEM)
SMEM = pl.BlockSpec(memory_space=pltpu.SMEM)


def shift(value, axis, by):
    size = lax.axis_size(axis)
    return lax.ppermute(value, axis, [(i, (i + by) % size) for i in range(size)])


def ring_gather(value, axis, first_half, second_half):
    before = shift(value, axis, 1)
    after = shift(value, axis, 3)
    far_first = shift(first_half(before), axis, 1)
    far_second = shift(second_half(after), axis, 3)
    return before, after, far_first, far_second


def gather_directly(value, axis):
    return tuple(shift(value, axis, by) for by in (1, 3, 2))


def call(kernel, args, out_shape, vmem_mib, cost=None, **kw):
    placed = [a if a.dtype == jnp.int32 else pltpu.with_memory_space_constraint(a, pltpu.VMEM) for a in args]
    return pl.pallas_call(
        kernel,
        in_specs=[SMEM if a.dtype == jnp.int32 else VMEM for a in args],
        out_specs=jax.tree.map(lambda _: VMEM, out_shape),
        out_shape=jax.tree.map(lambda o: pltpu.VMEM(o.shape, o.dtype), out_shape),
        compiler_params=pltpu.CompilerParams(vmem_limit_bytes=vmem_mib << 20),
        cost_estimate=cost,
        **kw,
    )(*placed)


def array(shape, dtype):
    return jax.ShapeDtypeStruct(shape, dtype)


def sums_kernel(tokens, gain, bias, out):
    x = tokens[...]
    ones = jnp.ones((8, x.shape[1]), BF16)
    add = lambda v: lax.dot_general(ones, v, (((1,), (1,)), ((), ())), preferred_element_type=F32)[0:1]
    square = x.astype(F32) * x.astype(F32)
    high = square.astype(BF16)
    low = (square - high.astype(F32)).astype(BF16)
    out[0:1, :] = add(x)
    out[1:2, :] = add(high) + add(low)
    width = gain.shape[1]
    out[2:4, :] = jnp.zeros((2, out.shape[1]), F32)
    out[2:3, :width] = gain[...].astype(F32)
    out[3:4, :width] = bias[...].astype(F32)


def project_kernel(ids, facts, facts_away, other, *refs):
    away, near, (w_hbm, keep, send, blocks, normed, w, stats, block_sems, sems) = refs[:4], refs[4:8], refs[8:]
    _, rows, width = blocks.shape
    half, n = rows // 2, w.shape[3]
    copies = {}
    for i, source in enumerate(near):
        copies[i] = pltpu.make_async_copy(source, blocks.at[i], block_sems.at[i])
        copies[i].start()
    for j in range(3):
        for part in range(2):
            first = pl.multiple_of((ids[0] if part == 0 else 1 - ids[0]) * 4 * width, HD)
            copies[j, part] = pltpu.make_async_copy(
                w_hbm.at[j, pl.ds(first, 4 * width)], w.at[j, part], sems.at[j, part]
            )
            copies[j, part].start()

    sums = other[...]
    for i in range(4):
        sums = sums + facts[i, 0:2] + facts_away[i, 0:2]
    mean = sums[0:1] / D
    inv = lax.rsqrt(sums[1:2] / D - mean * mean + EPS)
    stats[...] = jnp.concatenate([mean, inv, jnp.zeros((6, rows), F32)]).T
    for i in range(4):
        copies[i].wait()
    chunk = rows // 8

    def normalize(c, carry):
        at_rows = pl.ds(pl.multiple_of(c * chunk, chunk), chunk)
        mean, inv = stats[at_rows, 0:1], stats[at_rows, 1:2]
        for part, known in enumerate((facts, facts_away)):
            for i in range(4):
                at = pl.ds(pl.multiple_of(ids[1 + i] * width, HD), width)
                gain, bias = known[i, 2:3, :width], known[i, 3:4, :width]
                x = (blocks[i, at_rows] if part == 0 else away[i][at_rows]).astype(F32)
                normed[part, at_rows, at] = ((x - mean) * inv * gain + bias).astype(BF16)
        return carry

    lax.fori_loop(0, 8, normalize, 0)
    row = ids[5]

    def columns_of(j, carry):
        cols = pl.ds(pl.multiple_of(j * n, n), n)
        for part in range(2):
            first = pl.multiple_of((ids[0] if part == 0 else 1 - ids[0]) * 4 * width, HD)
            pltpu.make_async_copy(
                w_hbm.at[j, pl.ds(first, 4 * width)], w.at[j, part], sems.at[j, part]
            ).wait()
        total = jnp.dot(normed[0], w[j, 0], preferred_element_type=F32)
        total = total + jnp.dot(normed[1], w[j, 1], preferred_element_type=F32)
        first, second = total[:half], total[half:]
        keep[:, cols] = jnp.where(row == 0, first, second)
        send[:, cols] = jnp.where(row == 0, second, first).astype(send.dtype)
        return carry

    lax.fori_loop(0, 3, columns_of, 0)


def project(ids, near, away, facts, facts_away, other, w_qkv):
    rows, width = near[0].shape
    n = w_qkv.shape[2]
    args = [pltpu.with_memory_space_constraint(v, pltpu.VMEM) for v in (facts, facts_away, other, *away)]
    args += [pltpu.with_memory_space_constraint(v, pltpu.HBM) for v in (*near, w_qkv)]
    return pl.pallas_call(
        project_kernel,
        in_specs=[SMEM] + [VMEM] * 7 + [pl.BlockSpec(memory_space=pltpu.HBM)] * 5,
        out_specs=[VMEM] * 2,
        scratch_shapes=[
            pltpu.VMEM((4, rows, width), BF16),
            pltpu.VMEM((2, rows, 4 * width), BF16),
            pltpu.VMEM((3, 2, 4 * width, n), BF16),
            pltpu.VMEM((rows, 8), F32),
            pltpu.SemaphoreType.DMA((4,)),
            pltpu.SemaphoreType.DMA((3, 2)),
        ],
        out_shape=[pltpu.VMEM((rows // 2, 3 * n), t) for t in (F32, BF16)],
        compiler_params=pltpu.CompilerParams(vmem_limit_bytes=28 << 20),
        cost_estimate=pl.CostEstimate(flops=48 * rows * width * n, bytes_accessed=48 * width * n, transcendentals=0),
        name="project",
    )(ids, *args)


def split_kernel(zl, keep, recv, *outs):
    def step(j, carry):
        for s in range(4):
            head = lax.rem(zl[0] + s, 4)
            cols = pl.ds(pl.multiple_of(j * 512 + head * HD, HD), HD)
            outs[s][j] = (keep[:, cols] + recv[:, cols].astype(F32)).astype(BF16)
        return carry

    lax.fori_loop(0, 3, step, 0)


def split_heads(zl, keep, recv):
    return call(split_kernel, (zl, keep, recv), [array((3, keep.shape[0], HD), BF16)] * 4, 8)


def attend_kernel(n_kv, first, last, *refs):
    q_ref, *refs = refs
    kvs, refs = refs[: 2 * n_kv], refs[2 * n_kv :]
    if not first:
        (m_in, l_in, a_in), refs = refs[:3], refs[3:]
    outs = refs
    keys = [r[...].reshape(-1, HD) for r in kvs[0::2]]
    values = [r[...].reshape(-1, HD) for r in kvs[1::2]]
    size = q_ref.shape[1] // SPLIT

    def tile(step, carry):
        at = step // SPLIT, pl.ds(pl.multiple_of(step % SPLIT * size, size), size)
        q = q_ref[at]
        scores = [
            lax.dot_general(q, k, (((1,), (1,)), ((), ())), preferred_element_type=F32) for k in keys
        ]
        top = functools.reduce(jnp.maximum, [jnp.max(s, axis=1, keepdims=True) for s in scores])
        if not first:
            top = jnp.maximum(m_in[at][:, :1], top)
        base = top * SCORE_LOG2
        partial_sum = None
        weighted = None
        for s, v in zip(scores, values):
            p = jnp.exp2(s * SCORE_LOG2 - base)
            for c in range(0, p.shape[1], HD):
                piece = p[:, c : c + HD]
                partial_sum = piece if partial_sum is None else partial_sum + piece
            pv = jnp.dot(p.astype(BF16), v, preferred_element_type=F32)
            weighted = pv if weighted is None else weighted + pv
        if not first:
            shrink = jnp.exp2(m_in[at][:, :1] * SCORE_LOG2 - base)
            partial_sum = partial_sum + l_in[at] * shrink
            weighted = weighted + a_in[at] * shrink
        if last:
            total = jnp.sum(partial_sum, axis=1, keepdims=True)
            outs[0][at] = (weighted / total).astype(BF16)
        else:
            outs[0][at] = jnp.broadcast_to(top, weighted.shape)
            outs[1][at] = partial_sum
            outs[2][at] = weighted
        return carry

    lax.fori_loop(0, 4 * SPLIT, tile, 0, unroll=2 if last else 1)


def attend(q, kvs, state, last):
    rows = q.shape[1]
    n_keys = sum(k.size // HD for k, _ in kvs)
    args = [q]
    for k, v in kvs:
        args += [k, v]
    first = state is None
    if not first:
        args += list(state)
    out_shape = [array((4, rows, HD), BF16)] if last else [array((4, rows, HD), F32)] * 3
    cost = pl.CostEstimate(
        flops=16 * rows * n_keys * HD * 2, bytes_accessed=4 * n_keys * HD, transcendentals=4 * rows * n_keys
    )
    return call(functools.partial(attend_kernel, len(kvs), first, last), args, out_shape, 36, cost)


def join_kernel(zl, c0, c1, c2, c3, out):
    for s, c in enumerate((c0, c1, c2, c3)):
        head = lax.rem(zl[0] + s, 4)
        out[:, pl.ds(pl.multiple_of(head * HD, HD), HD)] = c[...]


def join_heads(zl, parts):
    return call(join_kernel, (zl, *parts), array((parts[0].shape[0], 4 * HD), BF16), 4)


def mix(own, rest, weights, which):
    total = jnp.dot(own[...], weights[0][which], preferred_element_type=F32)
    for i, w in ((0, 1), (1, 3), (2, 2)):
        total = total + jnp.dot(rest[i], weights[w][which], preferred_element_type=F32)
    return total


def mix_send_kernel(own, rest, *refs):
    refs[4][...] = mix(own, rest, refs[:4], 1).astype(BF16)


def mix_send(contexts, weights):
    rows, width = contexts[0].shape[0], weights[0].shape[2]
    cost = pl.CostEstimate(flops=2 * rows * 2048 * width, bytes_accessed=4096 * width, transcendentals=0)
    return call(mix_send_kernel, (*contexts, *weights), array((rows, width), BF16), 12, cost)


def mix_own_kernel(own, rest, other, other_rest, *refs):
    refs[4][0] = mix(own, rest, refs[:4], 0)
    refs[4][1] = mix(other, other_rest, refs[:4], 0)


def mix_own(own, other, weights):
    rows, width = own[0].shape[0], weights[0].shape[2]
    cost = pl.CostEstimate(flops=4 * rows * 2048 * width, bytes_accessed=4096 * width, transcendentals=0)
    return call(mix_own_kernel, (*own, *other, *weights), array((2, rows, width), F32), 12, cost)


def finish_kernel(row, tokens, own, first, second, out):
    half = tokens.shape[0] // 2
    for i, received in ((0, first), (1, second)):
        at = row[0] if i == 0 else 1 - row[0]
        rows = pl.ds(pl.multiple_of(at * half, half), half)
        out[rows, :] = (tokens[rows, :].astype(F32) + own[i] + received[...].astype(F32)).astype(BF16)


def finish(row, tokens, own, first, second):
    return pl.pallas_call(
        finish_kernel,
        in_specs=[SMEM] + [VMEM] * 4,
        out_specs=VMEM,
        out_shape=array(tokens.shape, BF16),
        name="finish",
    )(row, *(pltpu.with_memory_space_constraint(v, pltpu.VMEM) for v in (tokens, own, first, second)))


def layer(tokens, ln_gain, ln_bias, w_qkv, w_out):
    row, zh, y, zl = (lax.axis_index(a) for a in ("row", "zh", "y", "zl"))
    as_int = lambda *v: jnp.stack([jnp.asarray(u, jnp.int32) for u in v])
    rows, width = tokens.shape

    partner = shift(tokens, "zh", 1)
    near = gather_directly(tokens, "y")
    local = call(sums_kernel, (tokens, ln_gain[None, :], ln_bias[None, :]), array((4, rows), F32), 8)
    facts = jnp.stack([local, *gather_directly(local, "y")])
    facts_away = shift(facts, "zh", 1)
    other = shift(jnp.sum(facts[:, 0:2] + facts_away[:, 0:2], axis=0), "row", 1)
    away = gather_directly(partner, "y")
    order = (y, (y + 3) % 4, (y + 1) % 4, (y + 2) % 4)
    keep, send = project(
        as_int(zh, *order, row), (tokens, *near), (partner, *away), facts, facts_away, other, w_qkv
    )
    recv = shift(send, "row", 1)

    zl_arr = as_int(zl)
    slabs = split_heads(zl_arr, keep, recv)
    slabs = [slabs[0]] + [shift(slabs[s], "zl", s) for s in (1, 2, 3)]
    queries = jnp.stack([s[0] for s in slabs])
    kv = jnp.stack([s[1:] for s in slabs], axis=1)

    w_out, _ = lax.optimization_barrier((w_out, keep))
    columns = lambda z, s: lax.dynamic_slice_in_dim(w_out, (z * 4 + (y + s) % 4) * width, width, 1)
    weights = [jnp.stack([columns(zh, s), columns(1 - zh, s)]) for s in range(4)]
    weights = [weights[0]] + [shift(weights[s], "y", s) for s in (1, 2, 3)]

    before, after, far_k, far_v = ring_gather(kv, "x", lambda v: v[0], lambda v: v[1])
    swap = lambda v: shift(v, "row", 1)
    kv2 = swap(kv)
    before2 = swap(before)
    after2 = swap(after)
    far_k2 = swap(far_k)
    far_v2 = swap(far_v)
    pair = lambda v: (v[0], v[1])
    state = attend(queries, [pair(kv), pair(kv2)], None, False)
    state = attend(queries, [pair(before), pair(after)], state, False)
    state = attend(queries, [pair(before2), pair(after2)], state, False)
    contexts = attend(queries, [(far_k, far_v), (far_k2, far_v2)], state, True)[0]

    contexts = [contexts[0]] + [shift(contexts[s], "zl", 4 - s) for s in (1, 2, 3)]
    context = join_heads(zl_arr, contexts)
    own = (context, jnp.stack(gather_directly(context, "y")))
    other = tuple(swap(v) for v in own)
    first = shift(mix_send(own, weights), "zh", 1)
    second = shift(mix_send(other, weights), "zh", 1)
    own_sum = mix_own(own, other, weights)
    return finish(as_int(row), tokens, own_sum, first, second)


def solution(mesh):
    finer = Mesh(mesh.devices.reshape(4, 4, 2, 2, 4), ("x", "zl", "row", "zh", "y"))
    feature = ("row", "zh", "y")
    in_specs = (
        P(("x", "zl"), feature),
        P(feature),
        P(feature),
        P(None, "row", ("zh", "y")),
        P(("zh", "y"), "row"),
    )
    return jax.shard_map(layer, mesh=finer, in_specs=in_specs, out_specs=P(("x", "zl"), feature), check_vma=False)
```

profile of v0, /device:TPU:1, one launch (start us, length us, event | category | flops | bytes accessed | tf_op | source)
XLA Modules:
  0.0 219.0 jit_solution(16114577782893529208)
XLA Ops:
  0.0 7.7 %collective-permute-start.5 = (bf16[512,384]{1,0:T(8,128)(2,1)}, bf16[512,384]{1,0:T(8,128)(2,1)S(1)}, u32[]{:S(2)}, u32[]{:S(2)}) collective-permute-start(bf16[512,384]{1,0:T(8,128)(2,1)} %tokens.3), channel_id=1, source_target_pairs={{0,4},{4,0},{1,5},{5,1},{2,6},{6,2},{3,7},{7,3},{8,12},{12,8},{9,1... | collective-permute-start | bytes 1179656 | tf_op jit(solution)/shard_map/ppermute | solution.py:25
  7.7 2.9 %collective-permute-start.11 = (bf16[512,384]{1,0:T(8,128)(2,1)}, bf16[512,384]{1,0:T(8,128)(2,1)}, u32[]{:S(2)}, u32[]{:S(2)}) collective-permute-start(bf16[512,384]{1,0:T(8,128)(2,1)} %tokens.3), channel_id=1, source_target_pairs={{0,2},{1,3},{2,0},{3,1},{4,6},{5,7},{6,4},{7,5},{8,10},{9,11},{10,... | collective-permute-start | bytes 1179656 | tf_op jit(solution)/shard_map/ppermute | solution.py:25
  12.0 1.0 copy-done
  13.5 2.7 %collective-permute-start.1 = (f32[4,512]{1,0:T(4,128)S(1)}, f32[4,512]{1,0:T(4,128)S(1)}, u32[]{:S(2)}, u32[]{:S(2)}) collective-permute-start(f32[4,512]{1,0:T(4,128)S(1)} %shard_map.55), channel_id=1, source_target_pairs={{0,3},{1,0},{2,1},{3,2},{4,7},{5,4},{6,5},{7,6},{8,11},{9,8},{10,9... | collective-permute-start | bytes 24584 | tf_op jit(solution)/shard_map/ppermute | solution.py:25
  16.2 3.3 %collective-permute-done.2 = f32[4,512]{1,0:T(4,128)S(1)} collective-permute-done((f32[4,512]{1,0:T(4,128)S(1)}, f32[4,512]{1,0:T(4,128)S(1)}, u32[]{:S(2)}, u32[]{:S(2)}) %collective-permute-start.2) | collective-permute-done | bytes 8224 | tf_op jit(solution)/shard_map/ppermute | solution.py:25
  20.0 0.9 collective-permute-done
  21.1 10.0 %collective-permute-done.3.facts_away = f32[4,4,512]{2,1,0:T(4,128)S(1)} collective-permute-done((f32[4,4,512]{2,1,0:T(4,128)S(1)}, f32[4,4,512]{2,1,0:T(4,128)S(1)}, u32[]{:S(2)}, u32[]{:S(2)}) %collective-permute-start.3) | collective-permute-done | bytes 32800 | tf_op jit(solution)/shard_map/ppermute | solution.py:25
  31.7 3.1 %collective-permute-start.10 = (bf16[512,384]{1,0:T(8,128)(2,1)}, bf16[512,384]{1,0:T(8,128)(2,1)S(1)}, u32[]{:S(2)}, u32[]{:S(2)}) collective-permute-start(bf16[512,384]{1,0:T(8,128)(2,1)} %tokens.3), channel_id=1, source_target_pairs={{0,3},{1,0},{2,1},{3,2},{4,7},{5,4},{6,5},{7,6},{8,11},{9,8},{10,9... | collective-permute-start | bytes 1179656 | tf_op jit(solution)/shard_map/ppermute | solution.py:25
  34.8 1.6 collective-permute-start.8
  36.4 1.1 collective-permute-start.7
  38.2 13.5 %collective-permute-done.10.refs_6_ = bf16[512,384]{1,0:T(8,128)(2,1)S(1)} collective-permute-done((bf16[512,384]{1,0:T(8,128)(2,1)}, bf16[512,384]{1,0:T(8,128)(2,1)S(1)}, u32[]{:S(2)}, u32[]{:S(2)}) %collective-permute-start.10) | collective-permute-done | bytes 393248 | tf_op jit(solution)/shard_map/ppermute | solution.py:25
  51.7 2.5 %collective-permute-done.9.refs_5_ = bf16[512,384]{1,0:T(8,128)(2,1)S(1)} collective-permute-done((bf16[512,384]{1,0:T(8,128)(2,1)}, bf16[512,384]{1,0:T(8,128)(2,1)S(1)}, u32[]{:S(2)}, u32[]{:S(2)}) %collective-permute-start.9) | collective-permute-done | bytes 393248 | tf_op jit(solution)/shard_map/ppermute | solution.py:25
  54.2 6.0 %collective-permute-done.7.refs_2_ = bf16[512,384]{1,0:T(8,128)(2,1)S(1)} collective-permute-done((bf16[512,384]{1,0:T(8,128)(2,1)S(1)}, bf16[512,384]{1,0:T(8,128)(2,1)S(1)}, u32[]{:S(2)}, u32[]{:S(2)}) %collective-permute-start.7) | collective-permute-done | bytes 393248 | tf_op jit(solution)/shard_map/ppermute | solution.py:25
  61.0 2.4 %collective-permute-done.6.refs_1_ = bf16[512,384]{1,0:T(8,128)(2,1)S(1)} collective-permute-done((bf16[512,384]{1,0:T(8,128)(2,1)S(1)}, bf16[512,384]{1,0:T(8,128)(2,1)S(1)}, u32[]{:S(2)}, u32[]{:S(2)}) %collective-permute-start.6) | collective-permute-done | bytes 393248 | tf_op jit(solution)/shard_map/ppermute | solution.py:25
  64.1 1.0 copy-done.3
  65.1 1.0 copy-done.5
  66.1 11.6 %project.1 = (f32[256,1536]{1,0:T(8,128)S(1)}, bf16[256,1536]{1,0:T(8,128)(2,1)S(1)}) custom-call(s32[6]{0:T(128)S(1)} %stack.113.ids, f32[4,4,512]{2,1,0:T(4,128)S(1)} %pad_maximum_fusion.7.facts, f32[4,4,512]{2,1,0:T(4,128)S(1)} %collective-permute-done.3.facts_away, f32[2,512]{1,0:T(2,128)S(1)} %collective-permute-done.4.other, ...), custom_call_target="tpu_custom_call" | custom-call | flops 4831838208 | bytes 9437184 | tf_op jit(solution)/shard_map/project/pallas_call | solution.py:134
  77.7 1.3 collective-permute-start.12
  79.0 1.9 collective-permute-done.12.recv
  81.3 1.2 collective-permute-start.14
  82.5 2.1 collective-permute-start.15
  84.6 4.7 %collective-permute-done.13 = bf16[3,256,128]{2,1,0:T(8,128)(2,1)S(1)} collective-permute-done((bf16[3,256,128]{2,1,0:T(8,128)(2,1)S(1)}, bf16[3,256,128]{2,1,0:T(8,128)(2,1)S(1)}, u32[]{:S(2)}, u32[]{:S(2)}) %collective-permute-start.13) | collective-permute-done | bytes 196640 | tf_op jit(solution)/shard_map/ppermute | solution.py:25
  89.3 7.6 %collective-permute-done.14 = bf16[3,256,128]{2,1,0:T(8,128)(2,1)S(1)} collective-permute-done((bf16[3,256,128]{2,1,0:T(8,128)(2,1)S(1)}, bf16[3,256,128]{2,1,0:T(8,128)(2,1)S(1)}, u32[]{:S(2)}, u32[]{:S(2)}) %collective-permute-start.14) | collective-permute-done | bytes 196640 | tf_op jit(solution)/shard_map/ppermute | solution.py:25
  97.0 2.6 %collective-permute-start.18 = (bf16[2,4,256,128]{3,2,1,0:T(8,128)(2,1)S(1)}, bf16[2,4,256,128]{3,2,1,0:T(8,128)(2,1)S(1)}, u32[]{:S(2)}, u32[]{:S(2)}) collective-permute-start(bf16[2,4,256,128]{3,2,1,0:T(8,128)(2,1)S(1)} %pad_maximum_fusion.5), channel_id=1, source_target_pairs={{0,192},{64,0},{128,64},{192,128},{1,193},{65,1},{129,65},{193,129... | collective-permute-start | bytes 1572872 | tf_op jit(solution)/shard_map/ppermute | solution.py:25
  100.1 2.4 %collective-permute-start.24 = (bf16[2,4,256,128]{3,2,1,0:T(8,128)(2,1)S(1)}, bf16[2,4,256,128]{3,2,1,0:T(8,128)(2,1)S(1)}, u32[]{:S(2)}, u32[]{:S(2)}) collective-permute-start(bf16[2,4,256,128]{3,2,1,0:T(8,128)(2,1)S(1)} %pad_maximum_fusion.5), channel_id=1, source_target_pairs={{0,8},{8,0},{1,9},{9,1},{2,10},{10,2},{3,11},{11,3},{4,12},{12,4},... | collective-permute-start | bytes 1572872 | tf_op jit(solution)/shard_map/ppermute | solution.py:25
  102.6 6.2 %collective-permute-done.18 = bf16[2,4,256,128]{3,2,1,0:T(8,128)(2,1)S(1)} collective-permute-done((bf16[2,4,256,128]{3,2,1,0:T(8,128)(2,1)S(1)}, bf16[2,4,256,128]{3,2,1,0:T(8,128)(2,1)S(1)}, u32[]{:S(2)}, u32[]{:S(2)}) %collective-permute-start.18) | collective-permute-done | bytes 524320 | tf_op jit(solution)/shard_map/ppermute | solution.py:25
  108.8 3.5 %collective-permute-start.19 = (bf16[4,256,128]{2,1,0:T(8,128)(2,1)S(1)}, bf16[4,256,128]{2,1,0:T(8,128)(2,1)S(1)}, u32[]{:S(2)}, u32[]{:S(2)}) collective-permute-start(bf16[4,256,128]{2,1,0:T(8,128)(2,1)S(1)} %get-tuple-element.50.refs_4_), channel_id=1, source_target_pairs={{0,192},{64,0},{128,64},{192,128},{1,193},{65,1},{129,65},{193,129... | collective-permute-start | bytes 786440 | tf_op jit(solution)/shard_map/ppermute | solution.py:25
  112.3 4.8 %collective-permute-done.16 = bf16[2,4,256,128]{3,2,1,0:T(8,128)(2,1)S(1)} collective-permute-done((bf16[2,4,256,128]{3,2,1,0:T(8,128)(2,1)S(1)}, bf16[2,4,256,128]{3,2,1,0:T(8,128)(2,1)S(1)}, u32[]{:S(2)}, u32[]{:S(2)}) %collective-permute-start.16) | collective-permute-done | bytes 524320 | tf_op jit(solution)/shard_map/ppermute | solution.py:25
  117.2 1.0 collective-permute-start.23
  118.4 4.2 %shard_map.57 = (f32[4,256,128]{2,1,0:T(8,128)S(1)}, f32[4,256,128]{2,1,0:T(8,128)S(1)}, f32[4,256,128]{2,1,0:T(8,128)S(1)}) custom-call(bf16[4,256,128]{2,1,0:T(8,128)(2,1)S(1)} %pad_maximum_fusion.6.refs_0_, bf16[4,256,128]{2,1,0:T(8,128)(2,1)S(1)} %get-tuple-element.48.refs_1_, bf16[4,256,128]{2,1,0:T(8,128)(2,1)S(1)} %get-tuple-element.47.refs_2_, ...), custom_call_target="tpu_custom_call" | custom-call | flops 2147483648 | bytes 1048576 | tf_op jit(solution)/shard_map/pallas_call | solution.py:42
  122.6 5.1 %shard_map.58 = (f32[4,256,128]{2,1,0:T(8,128)S(1)}, f32[4,256,128]{2,1,0:T(8,128)S(1)}, f32[4,256,128]{2,1,0:T(8,128)S(1)}) custom-call(bf16[4,256,128]{2,1,0:T(8,128)(2,1)S(1)} %pad_maximum_fusion.6.refs_0_, bf16[4,256,128]{2,1,0:T(8,128)(2,1)S(1)} %get-tuple-element.52.refs_1_, bf16[4,256,128]{2,1,0:T(8,128)(2,1)S(1)} %get-tuple-element.51.refs_2_, ...), custom_call_target="tpu_custom_call" | custom-call | flops 2147483648 | bytes 1048576 | tf_op jit(solution)/shard_map/pallas_call | solution.py:42
  128.6 5.1 %shard_map.59 = (f32[4,256,128]{2,1,0:T(8,128)S(1)}, f32[4,256,128]{2,1,0:T(8,128)S(1)}, f32[4,256,128]{2,1,0:T(8,128)S(1)}) custom-call(bf16[4,256,128]{2,1,0:T(8,128)(2,1)S(1)} %pad_maximum_fusion.6.refs_0_, bf16[4,256,128]{2,1,0:T(8,128)(2,1)S(1)} %get-tuple-element.56.refs_1_, bf16[4,256,128]{2,1,0:T(8,128)(2,1)S(1)} %get-tuple-element.55.refs_2_, ...), custom_call_target="tpu_custom_call" | custom-call | flops 2147483648 | bytes 1048576 | tf_op jit(solution)/shard_map/pallas_call | solution.py:42
  133.7 4.3 %shard_map.60 = bf16[4,256,128]{2,1,0:T(8,128)(2,1)S(1)} custom-call(bf16[4,256,128]{2,1,0:T(8,128)(2,1)S(1)} %pad_maximum_fusion.6.refs_0_, bf16[4,256,128]{2,1,0:T(8,128)(2,1)S(1)} %collective-permute-done.17.refs_1_, bf16[4,256,128]{2,1,0:T(8,128)(2,1)S(1)} %collective-permute-done.19.refs_2_, bf16[4,256,128]{2,1,0:T(8,128)(2,1)S(1)} %collective-permute-done.20.refs_3_, ...), custom_call_target="tpu_custom_call" | custom-call | flops 2147483648 | bytes 1048576 | tf_op jit(solution)/shard_map/pallas_call | solution.py:42
  138.1 3.7 %collective-permute-start.27 = (bf16[256,128]{1,0:T(8,128)(2,1)S(1)}, bf16[256,128]{1,0:T(8,128)(2,1)S(1)}, u32[]{:S(2)}, u32[]{:S(2)}) collective-permute-start(bf16[256,128]{1,0:T(8,128)(2,1)S(1)} %get-tuple-element.57), channel_id=1, source_target_pairs={{0,16},{16,32},{32,48},{48,0},{1,17},{17,33},{33,49},{49,1},{2,18}... | collective-permute-start | bytes 196616 | tf_op jit(solution)/shard_map/ppermute | solution.py:25
  141.8 2.2 collective-permute-start.25
  144.2 3.8 %collective-permute-done.26.c2 = bf16[256,128]{1,0:T(8,128)(2,1)S(1)} collective-permute-done((bf16[256,128]{1,0:T(8,128)(2,1)S(1)}, bf16[256,128]{1,0:T(8,128)(2,1)S(1)}, u32[]{:S(2)}, u32[]{:S(2)}) %collective-permute-start.26) | collective-permute-done | bytes 65568 | tf_op jit(solution)/shard_map/ppermute | solution.py:25
  148.2 1.2 collective-permute-start.29
  149.8 3.0 %collective-permute-start.34 = (bf16[2,512,384]{2,1,0:T(8,128)(2,1)S(1)}, bf16[2,512,384]{2,1,0:T(8,128)(2,1)S(1)}, u32[]{:S(2)}, u32[]{:S(2)}) collective-permute-start(bf16[2,512,384]{2,1,0:T(8,128)(2,1)S(1)} %pad_maximum_fusion.3), channel_id=1, source_target_pairs={{0,2},{1,3},{2,0},{3,1},{4,6},{5,7},{6,4},{7,5},{8,10},{9,11},{10,... | collective-permute-start | bytes 2359304 | tf_op jit(solution)/shard_map/ppermute | solution.py:25
  152.9 15.8 %collective-permute-done.30 = bf16[256,512]{1,0:T(8,128)(2,1)S(1)} collective-permute-done((bf16[256,512]{1,0:T(8,128)(2,1)S(1)}, bf16[256,512]{1,0:T(8,128)(2,1)S(1)}, u32[]{:S(2)}, u32[]{:S(2)}) %collective-permute-start.30) | collective-permute-done | bytes 262176 | tf_op jit(solution)/shard_map/ppermute | solution.py:25
  168.7 7.0 %collective-permute-done.28 = bf16[256,512]{1,0:T(8,128)(2,1)S(1)} collective-permute-done((bf16[256,512]{1,0:T(8,128)(2,1)S(1)}, bf16[256,512]{1,0:T(8,128)(2,1)S(1)}, u32[]{:S(2)}, u32[]{:S(2)}) %collective-permute-start.28) | collective-permute-done | bytes 262176 | tf_op jit(solution)/shard_map/ppermute | solution.py:25
  175.8 17.9 %collective-permute-start.32 = (bf16[3,256,512]{2,1,0:T(8,128)(2,1)S(1)}, bf16[3,256,512]{2,1,0:T(8,128)(2,1)S(1)}, u32[]{:S(2)}, u32[]{:S(2)}) collective-permute-start(bf16[3,256,512]{2,1,0:T(8,128)(2,1)S(1)} %pad_maximum_fusion.rest), channel_id=1, source_target_pairs={{0,8},{8,0},{1,9},{9,1},{2,10},{10,2},{3,11},{11,3},{4,12},{12,4},... | collective-permute-start | bytes 2359304 | tf_op jit(solution)/shard_map/ppermute | solution.py:25
  193.8 0.9 collective-permute-done.35.refs_3_
  195.4 1.6 collective-permute-start.36
  197.7 4.2 %collective-permute-start.37 = (bf16[256,384]{1,0:T(8,128)(2,1)S(1)}, bf16[256,384]{1,0:T(8,128)(2,1)S(1)}, u32[]{:S(2)}, u32[]{:S(2)}) collective-permute-start(bf16[256,384]{1,0:T(8,128)(2,1)S(1)} %shard_map.64), channel_id=1, source_target_pairs={{0,4},{4,0},{1,5},{5,1},{2,6},{6,2},{3,7},{7,3},{8,12},{12,8},{9,1... | collective-permute-start | bytes 589832 | tf_op jit(solution)/shard_map/ppermute | solution.py:25
  202.0 1.2 shard_map.62.own
  203.2 6.2 %collective-permute-done.36.first = bf16[256,384]{1,0:T(8,128)(2,1)S(1)} collective-permute-done((bf16[256,384]{1,0:T(8,128)(2,1)S(1)}, bf16[256,384]{1,0:T(8,128)(2,1)S(1)}, u32[]{:S(2)}, u32[]{:S(2)}) %collective-permute-start.36) | collective-permute-done | bytes 196640 | tf_op jit(solution)/shard_map/ppermute | solution.py:25
  209.4 8.7 %collective-permute-done.37.second = bf16[256,384]{1,0:T(8,128)(2,1)S(1)} collective-permute-done((bf16[256,384]{1,0:T(8,128)(2,1)S(1)}, bf16[256,384]{1,0:T(8,128)(2,1)S(1)}, u32[]{:S(2)}, u32[]{:S(2)}) %collective-permute-start.37) | collective-permute-done | bytes 196640 | tf_op jit(solution)/shard_map/ppermute | solution.py:25
  218.2 0.9 finish.1
  (86 shorter events, 10.2 us)
Async XLA Ops:
  0.0 34.8 %collective-permute-start.5 = (bf16[512,384]{1,0:T(8,128)(2,1)}, bf16[512,384]{1,0:T(8,128)(2,1)S(1)}, u32[]{:S(2)}, u32[]{:S(2)}) collective-permute-start(bf16[512,384]{1,0:T(8,128)(2,1)} %tokens.3), channel_id=1, source_target_pairs={{0,4},{4,0},{1,5},{5,1},{2,6},{6,2},{3,7},{7,3},{8,12},{12,8},{9,1... | collective-permute-start | bytes 1179656 | tf_op jit(solution)/shard_map/ppermute | solution.py:25
  7.7 29.8 %collective-permute-start.11 = (bf16[512,384]{1,0:T(8,128)(2,1)}, bf16[512,384]{1,0:T(8,128)(2,1)}, u32[]{:S(2)}, u32[]{:S(2)}) collective-permute-start(bf16[512,384]{1,0:T(8,128)(2,1)} %tokens.3), channel_id=1, source_target_pairs={{0,2},{1,3},{2,0},{3,1},{4,6},{5,7},{6,4},{7,5},{8,10},{9,11},{10,... | collective-permute-start | bytes 1179656 | tf_op jit(solution)/shard_map/ppermute | solution.py:25
  12.0 1.0 copy-start
  13.4 6.1 %collective-permute-start.2 = (f32[4,512]{1,0:T(4,128)S(1)}, f32[4,512]{1,0:T(4,128)S(1)}, u32[]{:S(2)}, u32[]{:S(2)}) collective-permute-start(f32[4,512]{1,0:T(4,128)S(1)} %shard_map.55), channel_id=1, source_target_pairs={{0,2},{1,3},{2,0},{3,1},{4,6},{5,7},{6,4},{7,5},{8,10},{9,11},{10,... | collective-permute-start | bytes 24584 | tf_op jit(solution)/shard_map/ppermute | solution.py:25
  13.5 6.5 %collective-permute-start.1 = (f32[4,512]{1,0:T(4,128)S(1)}, f32[4,512]{1,0:T(4,128)S(1)}, u32[]{:S(2)}, u32[]{:S(2)}) collective-permute-start(f32[4,512]{1,0:T(4,128)S(1)} %shard_map.55), channel_id=1, source_target_pairs={{0,3},{1,0},{2,1},{3,2},{4,7},{5,4},{6,5},{7,6},{8,11},{9,8},{10,9... | collective-permute-start | bytes 24584 | tf_op jit(solution)/shard_map/ppermute | solution.py:25
  16.2 4.7 %collective-permute-start = (f32[4,512]{1,0:T(4,128)S(1)}, f32[4,512]{1,0:T(4,128)S(1)}, u32[]{:S(2)}, u32[]{:S(2)}) collective-permute-start(f32[4,512]{1,0:T(4,128)S(1)} %shard_map.55), channel_id=1, source_target_pairs={{0,1},{1,2},{2,3},{3,0},{4,5},{5,6},{6,7},{7,4},{8,9},{9,10},{10,1... | collective-permute-start | bytes 24584 | tf_op jit(solution)/shard_map/ppermute | solution.py:25
  20.9 10.2 %collective-permute-start.3 = (f32[4,4,512]{2,1,0:T(4,128)S(1)}, f32[4,4,512]{2,1,0:T(4,128)S(1)}, u32[]{:S(2)}, u32[]{:S(2)}) collective-permute-start(f32[4,4,512]{2,1,0:T(4,128)S(1)} %pad_maximum_fusion.7.facts), channel_id=1, source_target_pairs={{0,4},{4,0},{1,5},{5,1},{2,6},{6,2},{3,7},{7,3},{8,12},{12,8},{9,1... | collective-permute-start | bytes 98312 | tf_op jit(solution)/shard_map/ppermute | solution.py:25
  31.1 5.3 %collective-permute-start.4 = (f32[2,512]{1,0:T(2,128)S(1)}, f32[2,512]{1,0:T(2,128)S(1)}, u32[]{:S(2)}, u32[]{:S(2)}) collective-permute-start(f32[2,512]{1,0:T(2,128)S(1)} %fusion), channel_id=1, source_target_pairs={{0,8},{8,0},{1,9},{9,1},{2,10},{10,2},{3,11},{11,3},{4,12},{12,4},... | collective-permute-start | bytes 12296 | tf_op jit(solution)/shard_map/ppermute | solution.py:25
  31.7 20.1 %collective-permute-start.10 = (bf16[512,384]{1,0:T(8,128)(2,1)}, bf16[512,384]{1,0:T(8,128)(2,1)S(1)}, u32[]{:S(2)}, u32[]{:S(2)}) collective-permute-start(bf16[512,384]{1,0:T(8,128)(2,1)} %tokens.3), channel_id=1, source_target_pairs={{0,3},{1,0},{2,1},{3,2},{4,7},{5,4},{6,5},{7,6},{8,11},{9,8},{10,9... | collective-permute-start | bytes 1179656 | tf_op jit(solution)/shard_map/ppermute | solution.py:25
  34.8 19.5 %collective-permute-start.9 = (bf16[512,384]{1,0:T(8,128)(2,1)}, bf16[512,384]{1,0:T(8,128)(2,1)S(1)}, u32[]{:S(2)}, u32[]{:S(2)}) collective-permute-start(bf16[512,384]{1,0:T(8,128)(2,1)} %tokens.3), channel_id=1, source_target_pairs={{0,1},{1,2},{2,3},{3,0},{4,5},{5,6},{6,7},{7,4},{8,9},{9,10},{10,1... | collective-permute-start | bytes 1179656 | tf_op jit(solution)/shard_map/ppermute | solution.py:25
  34.8 19.5 %collective-permute-start.8 = (bf16[512,384]{1,0:T(8,128)(2,1)S(1)}, bf16[512,384]{1,0:T(8,128)(2,1)S(1)}, u32[]{:S(2)}, u32[]{:S(2)}) collective-permute-start(bf16[512,384]{1,0:T(8,128)(2,1)S(1)} %collective-permute-done.5.refs_0_), channel_id=1, source_target_pairs={{0,2},{1,3},{2,0},{3,1},{4,6},{5,7},{6,4},{7,5},{8,10},{9,11},{10,... | collective-permute-start | bytes 1179656 | tf_op jit(solution)/shard_map/ppermute | solution.py:25
  36.4 23.8 %collective-permute-start.7 = (bf16[512,384]{1,0:T(8,128)(2,1)S(1)}, bf16[512,384]{1,0:T(8,128)(2,1)S(1)}, u32[]{:S(2)}, u32[]{:S(2)}) collective-permute-start(bf16[512,384]{1,0:T(8,128)(2,1)S(1)} %collective-permute-done.5.refs_0_), channel_id=1, source_target_pairs={{0,3},{1,0},{2,1},{3,2},{4,7},{5,4},{6,5},{7,6},{8,11},{9,8},{10,9... | collective-permute-start | bytes 1179656 | tf_op jit(solution)/shard_map/ppermute | solution.py:25
  37.5 25.8 %collective-permute-start.6 = (bf16[512,384]{1,0:T(8,128)(2,1)S(1)}, bf16[512,384]{1,0:T(8,128)(2,1)S(1)}, u32[]{:S(2)}, u32[]{:S(2)}) collective-permute-start(bf16[512,384]{1,0:T(8,128)(2,1)S(1)} %collective-permute-done.5.refs_0_), channel_id=1, source_target_pairs={{0,1},{1,2},{2,3},{3,0},{4,5},{5,6},{6,7},{7,4},{8,9},{9,10},{10,1... | collective-permute-start | bytes 1179656 | tf_op jit(solution)/shard_map/ppermute | solution.py:25
  51.7 8.5 %copy-start.7 = (bf16[512,384]{1,0:T(8,128)(2,1)}, bf16[512,384]{1,0:T(8,128)(2,1)S(1)}, u32[]{:S(2)}) copy-start(bf16[512,384]{1,0:T(8,128)(2,1)S(1)} %collective-permute-done.10.refs_6_) | copy-start | bytes 1179652
  54.2 6.0 %copy-start.8 = (bf16[512,384]{1,0:T(8,128)(2,1)}, bf16[512,384]{1,0:T(8,128)(2,1)S(1)}, u32[]{:S(2)}) copy-start(bf16[512,384]{1,0:T(8,128)(2,1)S(1)} %collective-permute-done.9.refs_5_) | copy-start | bytes 1179652
  60.2 0.8 copy-start.2
  63.3 0.7 copy-start.4
  64.1 1.0 copy-start.3
  65.1 1.0 copy-start.5
  77.7 3.2 %collective-permute-start.12 = (bf16[256,1536]{1,0:T(8,128)(2,1)S(1)}, bf16[256,1536]{1,0:T(8,128)(2,1)S(1)}, u32[]{:S(2)}, u32[]{:S(2)}) collective-permute-start(bf16[256,1536]{1,0:T(8,128)(2,1)S(1)} %get-tuple-element.22), channel_id=1, source_target_pairs={{0,8},{8,0},{1,9},{9,1},{2,10},{10,2},{3,11},{11,3},{4,12},{12,4},... | collective-permute-start | bytes 2359304 | tf_op jit(solution)/shard_map/ppermute | solution.py:25
  79.0 20.6 %copy-start.6 = (bf16[512,3072]{1,0:T(8,128)(2,1)S(1)}, bf16[512,3072]{1,0:T(8,128)(2,1)}, u32[]{:S(2)}) copy-start(bf16[512,3072]{1,0:T(8,128)(2,1)} %param.9) | copy-start | bytes 9437188
  81.2 8.1 %collective-permute-start.13 = (bf16[3,256,128]{2,1,0:T(8,128)(2,1)S(1)}, bf16[3,256,128]{2,1,0:T(8,128)(2,1)S(1)}, u32[]{:S(2)}, u32[]{:S(2)}) collective-permute-start(bf16[3,256,128]{2,1,0:T(8,128)(2,1)S(1)} %get-tuple-element.24), channel_id=1, source_target_pairs={{0,16},{16,32},{32,48},{48,0},{1,17},{17,33},{33,49},{49,1},{2,18}... | collective-permute-start | bytes 589832 | tf_op jit(solution)/shard_map/ppermute | solution.py:25
  81.3 15.6 %collective-permute-start.14 = (bf16[3,256,128]{2,1,0:T(8,128)(2,1)S(1)}, bf16[3,256,128]{2,1,0:T(8,128)(2,1)S(1)}, u32[]{:S(2)}, u32[]{:S(2)}) collective-permute-start(bf16[3,256,128]{2,1,0:T(8,128)(2,1)S(1)} %get-tuple-element.25), channel_id=1, source_target_pairs={{0,32},{16,48},{32,0},{48,16},{1,33},{17,49},{33,1},{49,17},{2,34}... | collective-permute-start | bytes 589832 | tf_op jit(solution)/shard_map/ppermute | solution.py:25
  82.5 14.4 %collective-permute-start.15 = (bf16[3,256,128]{2,1,0:T(8,128)(2,1)S(1)}, bf16[3,256,128]{2,1,0:T(8,128)(2,1)S(1)}, u32[]{:S(2)}, u32[]{:S(2)}) collective-permute-start(bf16[3,256,128]{2,1,0:T(8,128)(2,1)S(1)} %get-tuple-element.26), channel_id=1, source_target_pairs={{0,48},{16,0},{32,16},{48,32},{1,49},{17,1},{33,17},{49,33},{2,50}... | collective-permute-start | bytes 589832 | tf_op jit(solution)/shard_map/ppermute | solution.py:25
  97.0 11.8 %collective-permute-start.18 = (bf16[2,4,256,128]{3,2,1,0:T(8,128)(2,1)S(1)}, bf16[2,4,256,128]{3,2,1,0:T(8,128)(2,1)S(1)}, u32[]{:S(2)}, u32[]{:S(2)}) collective-permute-start(bf16[2,4,256,128]{3,2,1,0:T(8,128)(2,1)S(1)} %pad_maximum_fusion.5), channel_id=1, source_target_pairs={{0,192},{64,0},{128,64},{192,128},{1,193},{65,1},{129,65},{193,129... | collective-permute-start | bytes 1572872 | tf_op jit(solution)/shard_map/ppermute | solution.py:25
  100.1 18.3 %collective-permute-start.24 = (bf16[2,4,256,128]{3,2,1,0:T(8,128)(2,1)S(1)}, bf16[2,4,256,128]{3,2,1,0:T(8,128)(2,1)S(1)}, u32[]{:S(2)}, u32[]{:S(2)}) collective-permute-start(bf16[2,4,256,128]{3,2,1,0:T(8,128)(2,1)S(1)} %pad_maximum_fusion.5), channel_id=1, source_target_pairs={{0,8},{8,0},{1,9},{9,1},{2,10},{10,2},{3,11},{11,3},{4,12},{12,4},... | collective-permute-start | bytes 1572872 | tf_op jit(solution)/shard_map/ppermute | solution.py:25
  102.5 14.6 %collective-permute-start.16 = (bf16[2,4,256,128]{3,2,1,0:T(8,128)(2,1)S(1)}, bf16[2,4,256,128]{3,2,1,0:T(8,128)(2,1)S(1)}, u32[]{:S(2)}, u32[]{:S(2)}) collective-permute-start(bf16[2,4,256,128]{3,2,1,0:T(8,128)(2,1)S(1)} %pad_maximum_fusion.5), channel_id=1, source_target_pairs={{0,64},{64,128},{128,192},{192,0},{1,65},{65,129},{129,193},{193,1... | collective-permute-start | bytes 1572872 | tf_op jit(solution)/shard_map/ppermute | solution.py:25
  108.8 18.9 %collective-permute-start.19 = (bf16[4,256,128]{2,1,0:T(8,128)(2,1)S(1)}, bf16[4,256,128]{2,1,0:T(8,128)(2,1)S(1)}, u32[]{:S(2)}, u32[]{:S(2)}) collective-permute-start(bf16[4,256,128]{2,1,0:T(8,128)(2,1)S(1)} %get-tuple-element.50.refs_4_), channel_id=1, source_target_pairs={{0,192},{64,0},{128,64},{192,128},{1,193},{65,1},{129,65},{193,129... | collective-permute-start | bytes 786440 | tf_op jit(solution)/shard_map/ppermute | solution.py:25
  117.1 11.1 %collective-permute-start.17 = (bf16[4,256,128]{2,1,0:T(8,128)(2,1)S(1)}, bf16[4,256,128]{2,1,0:T(8,128)(2,1)S(1)}, u32[]{:S(2)}, u32[]{:S(2)}) collective-permute-start(bf16[4,256,128]{2,1,0:T(8,128)(2,1)S(1)} %get-tuple-element.52.refs_1_), channel_id=1, source_target_pairs={{0,64},{64,128},{128,192},{192,0},{1,65},{65,129},{129,193},{193,1... | collective-permute-start | bytes 786440 | tf_op jit(solution)/shard_map/ppermute | solution.py:25
  117.2 11.3 %collective-permute-start.23 = (bf16[2,4,256,128]{3,2,1,0:T(8,128)(2,1)S(1)}, bf16[2,4,256,128]{3,2,1,0:T(8,128)(2,1)S(1)}, u32[]{:S(2)}, u32[]{:S(2)}) collective-permute-start(bf16[2,4,256,128]{3,2,1,0:T(8,128)(2,1)S(1)} %collective-permute-done.18), channel_id=1, source_target_pairs={{0,8},{8,0},{1,9},{9,1},{2,10},{10,2},{3,11},{11,3},{4,12},{12,4},... | collective-permute-start | bytes 1572872 | tf_op jit(solution)/shard_map/ppermute | solution.py:25
  118.3 10.3 %collective-permute-start.22 = (bf16[2,4,256,128]{3,2,1,0:T(8,128)(2,1)S(1)}, bf16[2,4,256,128]{3,2,1,0:T(8,128)(2,1)S(1)}, u32[]{:S(2)}, u32[]{:S(2)}) collective-permute-start(bf16[2,4,256,128]{3,2,1,0:T(8,128)(2,1)S(1)} %collective-permute-done.16), channel_id=1, source_target_pairs={{0,8},{8,0},{1,9},{9,1},{2,10},{10,2},{3,11},{11,3},{4,12},{12,4},... | collective-permute-start | bytes 1572872 | tf_op jit(solution)/shard_map/ppermute | solution.py:25
  127.7 6.0 %collective-permute-start.21 = (bf16[4,256,128]{2,1,0:T(8,128)(2,1)S(1)}, bf16[4,256,128]{2,1,0:T(8,128)(2,1)S(1)}, u32[]{:S(2)}, u32[]{:S(2)}) collective-permute-start(bf16[4,256,128]{2,1,0:T(8,128)(2,1)S(1)} %collective-permute-done.19.refs_2_), channel_id=1, source_target_pairs={{0,8},{8,0},{1,9},{9,1},{2,10},{10,2},{3,11},{11,3},{4,12},{12,4},... | collective-permute-start | bytes 786440 | tf_op jit(solution)/shard_map/ppermute | solution.py:25
  128.2 5.5 %collective-permute-start.20 = (bf16[4,256,128]{2,1,0:T(8,128)(2,1)S(1)}, bf16[4,256,128]{2,1,0:T(8,128)(2,1)S(1)}, u32[]{:S(2)}, u32[]{:S(2)}) collective-permute-start(bf16[4,256,128]{2,1,0:T(8,128)(2,1)S(1)} %collective-permute-done.17.refs_1_), channel_id=1, source_target_pairs={{0,8},{8,0},{1,9},{9,1},{2,10},{10,2},{3,11},{11,3},{4,12},{12,4},... | collective-permute-start | bytes 786440 | tf_op jit(solution)/shard_map/ppermute | solution.py:25
  138.1 6.1 %collective-permute-start.27 = (bf16[256,128]{1,0:T(8,128)(2,1)S(1)}, bf16[256,128]{1,0:T(8,128)(2,1)S(1)}, u32[]{:S(2)}, u32[]{:S(2)}) collective-permute-start(bf16[256,128]{1,0:T(8,128)(2,1)S(1)} %get-tuple-element.57), channel_id=1, source_target_pairs={{0,16},{16,32},{32,48},{48,0},{1,17},{17,33},{33,49},{49,1},{2,18}... | collective-permute-start | bytes 196616 | tf_op jit(solution)/shard_map/ppermute | solution.py:25
  141.8 6.1 %collective-permute-start.26 = (bf16[256,128]{1,0:T(8,128)(2,1)S(1)}, bf16[256,128]{1,0:T(8,128)(2,1)S(1)}, u32[]{:S(2)}, u32[]{:S(2)}) collective-permute-start(bf16[256,128]{1,0:T(8,128)(2,1)S(1)} %get-tuple-element.58), channel_id=1, source_target_pairs={{0,32},{16,48},{32,0},{48,16},{1,33},{17,49},{33,1},{49,17},{2,34}... | collective-permute-start | bytes 196616 | tf_op jit(solution)/shard_map/ppermute | solution.py:25
  141.8 6.1 %collective-permute-start.25 = (bf16[256,128]{1,0:T(8,128)(2,1)S(1)}, bf16[256,128]{1,0:T(8,128)(2,1)S(1)}, u32[]{:S(2)}, u32[]{:S(2)}) collective-permute-start(bf16[256,128]{1,0:T(8,128)(2,1)S(1)} %get-tuple-element.59), channel_id=1, source_target_pairs={{0,48},{16,0},{32,16},{48,32},{1,49},{17,1},{33,17},{49,33},{2,50}... | collective-permute-start | bytes 196616 | tf_op jit(solution)/shard_map/ppermute | solution.py:25
  144.1 49.7 %collective-permute-start.33 = (bf16[2,512,384]{2,1,0:T(8,128)(2,1)S(1)}, bf16[2,512,384]{2,1,0:T(8,128)(2,1)S(1)}, u32[]{:S(2)}, u32[]{:S(2)}) collective-permute-start(bf16[2,512,384]{2,1,0:T(8,128)(2,1)S(1)} %pad_maximum_fusion.2), channel_id=1, source_target_pairs={{0,1},{1,2},{2,3},{3,0},{4,5},{5,6},{6,7},{7,4},{8,9},{9,10},{10,1... | collective-permute-start | bytes 2359304 | tf_op jit(solution)/shard_map/ppermute | solution.py:25
  148.1 20.6 %collective-permute-start.30 = (bf16[256,512]{1,0:T(8,128)(2,1)S(1)}, bf16[256,512]{1,0:T(8,128)(2,1)S(1)}, u32[]{:S(2)}, u32[]{:S(2)}) collective-permute-start(bf16[256,512]{1,0:T(8,128)(2,1)S(1)} %shard_map.61.own), channel_id=1, source_target_pairs={{0,2},{1,3},{2,0},{3,1},{4,6},{5,7},{6,4},{7,5},{8,10},{9,11},{10,... | collective-permute-start | bytes 786440 | tf_op jit(solution)/shard_map/ppermute | solution.py:25
  148.2 20.5 %collective-permute-start.29 = (bf16[256,512]{1,0:T(8,128)(2,1)S(1)}, bf16[256,512]{1,0:T(8,128)(2,1)S(1)}, u32[]{:S(2)}, u32[]{:S(2)}) collective-permute-start(bf16[256,512]{1,0:T(8,128)(2,1)S(1)} %shard_map.61.own), channel_id=1, source_target_pairs={{0,3},{1,0},{2,1},{3,2},{4,7},{5,4},{6,5},{7,6},{8,11},{9,8},{10,9... | collective-permute-start | bytes 786440 | tf_op jit(solution)/shard_map/ppermute | solution.py:25
  149.4 26.3 %collective-permute-start.28 = (bf16[256,512]{1,0:T(8,128)(2,1)S(1)}, bf16[256,512]{1,0:T(8,128)(2,1)S(1)}, u32[]{:S(2)}, u32[]{:S(2)}) collective-permute-start(bf16[256,512]{1,0:T(8,128)(2,1)S(1)} %shard_map.61.own), channel_id=1, source_target_pairs={{0,1},{1,2},{2,3},{3,0},{4,5},{5,6},{6,7},{7,4},{8,9},{9,10},{10,1... | collective-permute-start | bytes 786440 | tf_op jit(solution)/shard_map/ppermute | solution.py:25
  149.8 44.0 %collective-permute-start.34 = (bf16[2,512,384]{2,1,0:T(8,128)(2,1)S(1)}, bf16[2,512,384]{2,1,0:T(8,128)(2,1)S(1)}, u32[]{:S(2)}, u32[]{:S(2)}) collective-permute-start(bf16[2,512,384]{2,1,0:T(8,128)(2,1)S(1)} %pad_maximum_fusion.3), channel_id=1, source_target_pairs={{0,2},{1,3},{2,0},{3,1},{4,6},{5,7},{6,4},{7,5},{8,10},{9,11},{10,... | collective-permute-start | bytes 2359304 | tf_op jit(solution)/shard_map/ppermute | solution.py:25
  168.7 26.1 %collective-permute-start.35 = (bf16[2,512,384]{2,1,0:T(8,128)(2,1)S(1)}, bf16[2,512,384]{2,1,0:T(8,128)(2,1)S(1)}, u32[]{:S(2)}, u32[]{:S(2)}) collective-permute-start(bf16[2,512,384]{2,1,0:T(8,128)(2,1)S(1)} %pad_maximum_fusion.4), channel_id=1, source_target_pairs={{0,3},{1,0},{2,1},{3,2},{4,7},{5,4},{6,5},{7,6},{8,11},{9,8},{10,9... | collective-permute-start | bytes 2359304 | tf_op jit(solution)/shard_map/ppermute | solution.py:25
  175.8 21.2 %collective-permute-start.32 = (bf16[3,256,512]{2,1,0:T(8,128)(2,1)S(1)}, bf16[3,256,512]{2,1,0:T(8,128)(2,1)S(1)}, u32[]{:S(2)}, u32[]{:S(2)}) collective-permute-start(bf16[3,256,512]{2,1,0:T(8,128)(2,1)S(1)} %pad_maximum_fusion.rest), channel_id=1, source_target_pairs={{0,8},{8,0},{1,9},{9,1},{2,10},{10,2},{3,11},{11,3},{4,12},{12,4},... | collective-permute-start | bytes 2359304 | tf_op jit(solution)/shard_map/ppermute | solution.py:25
  193.6 3.4 %collective-permute-start.31 = (bf16[256,512]{1,0:T(8,128)(2,1)S(1)}, bf16[256,512]{1,0:T(8,128)(2,1)S(1)}, u32[]{:S(2)}, u32[]{:S(2)}) collective-permute-start(bf16[256,512]{1,0:T(8,128)(2,1)S(1)} %shard_map.61.own), channel_id=1, source_target_pairs={{0,8},{8,0},{1,9},{9,1},{2,10},{10,2},{3,11},{11,3},{4,12},{12,4},... | collective-permute-start | bytes 786440 | tf_op jit(solution)/shard_map/ppermute | solution.py:25
  195.4 14.0 %collective-permute-start.36 = (bf16[256,384]{1,0:T(8,128)(2,1)S(1)}, bf16[256,384]{1,0:T(8,128)(2,1)S(1)}, u32[]{:S(2)}, u32[]{:S(2)}) collective-permute-start(bf16[256,384]{1,0:T(8,128)(2,1)S(1)} %shard_map.63), channel_id=1, source_target_pairs={{0,4},{4,0},{1,5},{5,1},{2,6},{6,2},{3,7},{7,3},{8,12},{12,8},{9,1... | collective-permute-start | bytes 589832 | tf_op jit(solution)/shard_map/ppermute | solution.py:25
  197.7 20.4 %copy-start.1 = (bf16[512,384]{1,0:T(8,128)(2,1)S(1)}, bf16[512,384]{1,0:T(8,128)(2,1)}, u32[]{:S(2)}) copy-start(bf16[512,384]{1,0:T(8,128)(2,1)} %tokens.3) | copy-start | bytes 1179652
  197.7 20.4 %collective-permute-start.37 = (bf16[256,384]{1,0:T(8,128)(2,1)S(1)}, bf16[256,384]{1,0:T(8,128)(2,1)S(1)}, u32[]{:S(2)}, u32[]{:S(2)}) collective-permute-start(bf16[256,384]{1,0:T(8,128)(2,1)S(1)} %shard_map.64), channel_id=1, source_target_pairs={{0,4},{4,0},{1,5},{5,1},{2,6},{6,2},{3,7},{7,3},{8,12},{12,8},{9,1... | collective-permute-start | bytes 589832 | tf_op jit(solution)/shard_map/ppermute | solution.py:25
where the time goes:
time: 220 us; the launch traced here: 219 us
  waiting for transfers between devices  107 us (49%)
  starting transfers between devices  70.1 us (32%)
  Pallas kernels  34.6 us (16%)
  local copies, waits for them, and re-layouts  6.76 us (3%)
    ppermute x38, waiting for transfers between devices, shift(): lax.ppermute(value, axis, [(i, (i + by) % size) for i in range(size)])  107 us
    ppermute x38, starting transfers between devices, shift(): lax.ppermute(value, axis, [(i, (i + by) % size) for i in range(size)])  70.1 us
    pallas_call x10, Pallas kernels, call(): pl.pallas_call(kernel, in_specs=[SMEM if a.dtype == jnp.int32 else VMEM f...  22.2 us
    pallas_call x1, Pallas kernels, project(): pl.pallas_call(project_kernel, in_specs=[SMEM] + [VMEM] * 7 + [pl.BlockSp...  11.6 us
    unnamed x18, local copies, waits for them, and re-layouts  4.5 us
  transfers between devices with their start and end apart: 38, of which 19 were waited for; matrix products, arithmetic and copies ran while one was open for 1% of the time, Pallas kernels for 8%

commit v1 on v0

--- a/solution.py
+++ b/solution.py
@@ -151,28 +151,41 @@
 
 
 def split_kernel(zl, keep, recv, *outs):
+    def own(j, s):
+        head = lax.rem(zl[0] + s, 4)
+        cols = pl.ds(pl.multiple_of(j * 512 + head * HD, HD), HD)
+        return (keep[:, cols] + recv[:, cols].astype(F32)).astype(BF16)
+
+    for s in range(4):
+        outs[s][...] = own(0, s)
+
     def step(j, carry):
         for s in range(4):
-            head = lax.rem(zl[0] + s, 4)
-            cols = pl.ds(pl.multiple_of(j * 512 + head * HD, HD), HD)
-            outs[s][j] = (keep[:, cols] + recv[:, cols].astype(F32)).astype(BF16)
+            outs[4 + s][j] = own(1 + j, s)
         return carry
 
-    lax.fori_loop(0, 3, step, 0)
+    lax.fori_loop(0, 2, step, 0)
 
 
 def split_heads(zl, keep, recv):
-    return call(split_kernel, (zl, keep, recv), [array((3, keep.shape[0], HD), BF16)] * 4, 8)
-
-
-def attend_kernel(n_kv, first, last, *refs):
+    rows = keep.shape[0]
+    return call(split_kernel, (zl, keep, recv), [array((rows, HD), BF16)] * 4 + [array((2, rows, HD), BF16)] * 4, 8)
+
+
+def attend_kernel(n_arrays, first, last, *refs):
     q_ref, *refs = refs
-    kvs, refs = refs[: 2 * n_kv], refs[2 * n_kv :]
+    arrays, refs = refs[:n_arrays], refs[n_arrays:]
     if not first:
         (m_in, l_in, a_in), refs = refs[:3], refs[3:]
     outs = refs
-    keys = [r[...].reshape(-1, HD) for r in kvs[0::2]]
-    values = [r[...].reshape(-1, HD) for r in kvs[1::2]]
+    blocks = []
+    for r in arrays:
+        if len(r.shape) == 5:
+            blocks += [r[i, j] for i in range(r.shape[0]) for j in range(2)]
+        else:
+            blocks += [r[0], r[1]] if r.shape[0] == 2 else [r[...]]
+    keys = [v.reshape(-1, HD) for v in blocks[0::2]]
+    values = [v.reshape(-1, HD) for v in blocks[1::2]]
     size = q_ref.shape[1] // SPLIT
 
     def tile(step, carry):
@@ -207,15 +220,13 @@
             outs[2][at] = weighted
         return carry
 
-    lax.fori_loop(0, 4 * SPLIT, tile, 0, unroll=2 if last else 1)
-
-
-def attend(q, kvs, state, last):
+    lax.fori_loop(0, 4 * SPLIT, tile, 0, unroll=1)
+
+
+def attend(q, arrays, state, last):
     rows = q.shape[1]
-    n_keys = sum(k.size // HD for k, _ in kvs)
-    args = [q]
-    for k, v in kvs:
-        args += [k, v]
+    n_keys = sum(v.size for v in arrays) // (2 * HD)
+    args = [q, *arrays]
     first = state is None
     if not first:
         args += list(state)
@@ -223,7 +234,7 @@
     cost = pl.CostEstimate(
         flops=16 * rows * n_keys * HD * 2, bytes_accessed=4 * n_keys * HD, transcendentals=4 * rows * n_keys
     )
-    return call(functools.partial(attend_kernel, len(kvs), first, last), args, out_shape, 36, cost)
+    return call(functools.partial(attend_kernel, len(arrays), first, last), args, out_shape, 36, cost)
 
 
 def join_kernel(zl, c0, c1, c2, c3, out):
@@ -302,9 +313,11 @@
 
     zl_arr = as_int(zl)
     slabs = split_heads(zl_arr, keep, recv)
+    queries, slabs = slabs[:4], slabs[4:]
     slabs = [slabs[0]] + [shift(slabs[s], "zl", s) for s in (1, 2, 3)]
-    queries = jnp.stack([s[0] for s in slabs])
-    kv = jnp.stack([s[1:] for s in slabs], axis=1)
+    queries = [queries[0]] + [shift(queries[s], "zl", s) for s in (1, 2, 3)]
+    kv = jnp.stack(slabs, axis=1)
+    queries = jnp.stack(queries)
 
     w_out, _ = lax.optimization_barrier((w_out, keep))
     columns = lambda z, s: lax.dynamic_slice_in_dim(w_out, (z * 4 + (y + s) % 4) * width, width, 1)
@@ -314,15 +327,12 @@
     before, after, far_k, far_v = ring_gather(kv, "x", lambda v: v[0], lambda v: v[1])
     swap = lambda v: shift(v, "row", 1)
     kv2 = swap(kv)
-    before2 = swap(before)
-    after2 = swap(after)
-    far_k2 = swap(far_k)
-    far_v2 = swap(far_v)
-    pair = lambda v: (v[0], v[1])
-    state = attend(queries, [pair(kv), pair(kv2)], None, False)
-    state = attend(queries, [pair(before), pair(after)], state, False)
-    state = attend(queries, [pair(before2), pair(after2)], state, False)
-    contexts = attend(queries, [(far_k, far_v), (far_k2, far_v2)], state, True)[0]
+    near2 = swap(jnp.stack([before, after]))
+    far2 = swap(jnp.stack([far_k, far_v]))
+    state = attend(queries, [kv, kv2], None, False)
+    state = attend(queries, [before, after], state, False)
+    state = attend(queries, [near2], state, False)
+    contexts = attend(queries, [far_k, far_v, far2], state, True)[0]
 
     contexts = [contexts[0]] + [shift(contexts[s], "zl", 4 - s) for s in (1, 2, 3)]
     context = join_heads(zl_arr, contexts)

time: 220 us -> 222 us (level)
  starting transfers between devices: 70.1 us -> 76.3 us
  waiting for transfers between devices: 107 us -> 103 us
    ppermute x38 -> x39, starting transfers between devices: 70.1 us -> 76.3 us  [shift(): lax.ppermute(value, axis, [(i, (i + by) % size) for i in range(size)])]
    ppermute x38 -> x39, waiting for transfers between devices: 107 us -> 103 us  [shift(): lax.ppermute(value, axis, [(i, (i + by) % size) for i in range(size)])]
  transfers between devices with their start and end apart: 38 -> 39, of which waited for: 19 -> 22; matrix products, arithmetic and copies ran while one was open for 1% -> 1% of each run, Pallas kernels for 8% -> 8%
where the time goes in v1:
time: 222 us
  waiting for transfers between devices  103 us (46%)
  starting transfers between devices  76.3 us (34%)
  Pallas kernels  35.3 us (16%)
  local copies, waits for them, and re-layouts  6.56 us (3%)
    ppermute x39, waiting for transfers between devices, shift(): lax.ppermute(value, axis, [(i, (i + by) % size) for i in range(size)])  103 us
    ppermute x39, starting transfers between devices, shift(): lax.ppermute(value, axis, [(i, (i + by) % size) for i in range(size)])  76.3 us
    pallas_call x10, Pallas kernels, call(): pl.pallas_call(kernel, in_specs=[SMEM if a.dtype == jnp.int32 else VMEM f...  22.8 us
    pallas_call x1, Pallas kernels, project(): pl.pallas_call(project_kernel, in_specs=[SMEM] + [VMEM] * 7 + [pl.BlockSp...  11.6 us
    unnamed x18, local copies, waits for them, and re-layouts  4.54 us
  transfers between devices with their start and end apart: 39, of which 22 were waited for; matrix products, arithmetic and copies ran while one was open for 1% of the time, Pallas kernels for 8%

profile of v1, /device:TPU:1, one launch (start us, length us, event | category | flops | bytes accessed | tf_op | source)
XLA Modules:
  0.0 222.0 jit_solution(16453518525715766603)
XLA Ops:
  0.0 7.7 %collective-permute-start.5 = (bf16[512,384]{1,0:T(8,128)(2,1)}, bf16[512,384]{1,0:T(8,128)(2,1)S(1)}, u32[]{:S(2)}, u32[]{:S(2)}) collective-permute-start(bf16[512,384]{1,0:T(8,128)(2,1)} %tokens.3), channel_id=1, source_target_pairs={{0,4},{4,0},{1,5},{5,1},{2,6},{6,2},{3,7},{7,3},{8,12},{12,8},{9,1... | collective-permute-start | bytes 1179656 | tf_op jit(solution)/shard_map/ppermute | solution.py:25
  7.7 2.9 %collective-permute-start.11 = (bf16[512,384]{1,0:T(8,128)(2,1)}, bf16[512,384]{1,0:T(8,128)(2,1)}, u32[]{:S(2)}, u32[]{:S(2)}) collective-permute-start(bf16[512,384]{1,0:T(8,128)(2,1)} %tokens.3), channel_id=1, source_target_pairs={{0,2},{1,3},{2,0},{3,1},{4,6},{5,7},{6,4},{7,5},{8,10},{9,11},{10,... | collective-permute-start | bytes 1179656 | tf_op jit(solution)/shard_map/ppermute | solution.py:25
  12.0 1.0 copy-done
  13.5 2.7 %collective-permute-start.1 = (f32[4,512]{1,0:T(4,128)S(1)}, f32[4,512]{1,0:T(4,128)S(1)}, u32[]{:S(2)}, u32[]{:S(2)}) collective-permute-start(f32[4,512]{1,0:T(4,128)S(1)} %shard_map.55), channel_id=1, source_target_pairs={{0,3},{1,0},{2,1},{3,2},{4,7},{5,4},{6,5},{7,6},{8,11},{9,8},{10,9... | collective-permute-start | bytes 24584 | tf_op jit(solution)/shard_map/ppermute | solution.py:25
  16.2 3.3 %collective-permute-done.2 = f32[4,512]{1,0:T(4,128)S(1)} collective-permute-done((f32[4,512]{1,0:T(4,128)S(1)}, f32[4,512]{1,0:T(4,128)S(1)}, u32[]{:S(2)}, u32[]{:S(2)}) %collective-permute-start.2) | collective-permute-done | bytes 8224 | tf_op jit(solution)/shard_map/ppermute | solution.py:25
  21.1 10.0 %collective-permute-done.3.facts_away = f32[4,4,512]{2,1,0:T(4,128)S(1)} collective-permute-done((f32[4,4,512]{2,1,0:T(4,128)S(1)}, f32[4,4,512]{2,1,0:T(4,128)S(1)}, u32[]{:S(2)}, u32[]{:S(2)}) %collective-permute-start.3) | collective-permute-done | bytes 32800 | tf_op jit(solution)/shard_map/ppermute | solution.py:25
  31.7 3.1 %collective-permute-start.10 = (bf16[512,384]{1,0:T(8,128)(2,1)}, bf16[512,384]{1,0:T(8,128)(2,1)S(1)}, u32[]{:S(2)}, u32[]{:S(2)}) collective-permute-start(bf16[512,384]{1,0:T(8,128)(2,1)} %tokens.3), channel_id=1, source_target_pairs={{0,3},{1,0},{2,1},{3,2},{4,7},{5,4},{6,5},{7,6},{8,11},{9,8},{10,9... | collective-permute-start | bytes 1179656 | tf_op jit(solution)/shard_map/ppermute | solution.py:25
  34.8 1.6 collective-permute-start.8
  36.4 1.1 collective-permute-start.7
  38.2 13.5 %collective-permute-done.10.refs_6_ = bf16[512,384]{1,0:T(8,128)(2,1)S(1)} collective-permute-done((bf16[512,384]{1,0:T(8,128)(2,1)}, bf16[512,384]{1,0:T(8,128)(2,1)S(1)}, u32[]{:S(2)}, u32[]{:S(2)}) %collective-permute-start.10) | collective-permute-done | bytes 393248 | tf_op jit(solution)/shard_map/ppermute | solution.py:25
  51.7 2.5 %collective-permute-done.9.refs_5_ = bf16[512,384]{1,0:T(8,128)(2,1)S(1)} collective-permute-done((bf16[512,384]{1,0:T(8,128)(2,1)}, bf16[512,384]{1,0:T(8,128)(2,1)S(1)}, u32[]{:S(2)}, u32[]{:S(2)}) %collective-permute-start.9) | collective-permute-done | bytes 393248 | tf_op jit(solution)/shard_map/ppermute | solution.py:25
  54.2 6.0 %collective-permute-done.7.refs_2_ = bf16[512,384]{1,0:T(8,128)(2,1)S(1)} collective-permute-done((bf16[512,384]{1,0:T(8,128)(2,1)S(1)}, bf16[512,384]{1,0:T(8,128)(2,1)S(1)}, u32[]{:S(2)}, u32[]{:S(2)}) %collective-permute-start.7) | collective-permute-done | bytes 393248 | tf_op jit(solution)/shard_map/ppermute | solution.py:25
  61.0 2.3 %collective-permute-done.6.refs_1_ = bf16[512,384]{1,0:T(8,128)(2,1)S(1)} collective-permute-done((bf16[512,384]{1,0:T(8,128)(2,1)S(1)}, bf16[512,384]{1,0:T(8,128)(2,1)S(1)}, u32[]{:S(2)}, u32[]{:S(2)}) %collective-permute-start.6) | collective-permute-done | bytes 393248 | tf_op jit(solution)/shard_map/ppermute | solution.py:25
  64.1 1.0 copy-done.3
  65.1 1.0 copy-done.5
  66.1 11.6 %project.1 = (f32[256,1536]{1,0:T(8,128)S(1)}, bf16[256,1536]{1,0:T(8,128)(2,1)S(1)}) custom-call(s32[6]{0:T(128)S(1)} %stack.143.ids, f32[4,4,512]{2,1,0:T(4,128)S(1)} %pad_maximum_fusion.9.facts, f32[4,4,512]{2,1,0:T(4,128)S(1)} %collective-permute-done.3.facts_away, f32[2,512]{1,0:T(2,128)S(1)} %collective-permute-done.4.other, ...), custom_call_target="tpu_custom_call" | custom-call | flops 4831838208 | bytes 9437184 | tf_op jit(solution)/shard_map/project/pallas_call | solution.py:134
  77.6 1.3 collective-permute-start.12
  79.0 1.9 collective-permute-done.12.recv
  81.3 1.2 collective-permute-start.17
  82.5 2.1 collective-permute-start.18
  84.5 3.3 %collective-permute-done.16 = bf16[2,256,128]{2,1,0:T(8,128)(2,1)S(1)} collective-permute-done((bf16[2,256,128]{2,1,0:T(8,128)(2,1)S(1)}, bf16[2,256,128]{2,1,0:T(8,128)(2,1)S(1)}, u32[]{:S(2)}, u32[]{:S(2)}) %collective-permute-start.16) | collective-permute-done | bytes 131104 | tf_op jit(solution)/shard_map/ppermute | solution.py:25
  87.8 4.8 %collective-permute-done.17 = bf16[2,256,128]{2,1,0:T(8,128)(2,1)S(1)} collective-permute-done((bf16[2,256,128]{2,1,0:T(8,128)(2,1)S(1)}, bf16[2,256,128]{2,1,0:T(8,128)(2,1)S(1)}, u32[]{:S(2)}, u32[]{:S(2)}) %collective-permute-start.17) | collective-permute-done | bytes 131104 | tf_op jit(solution)/shard_map/ppermute | solution.py:25
  92.7 2.6 %collective-permute-start.21 = (bf16[2,4,256,128]{3,2,1,0:T(8,128)(2,1)S(1)}, bf16[2,4,256,128]{3,2,1,0:T(8,128)(2,1)S(1)}, u32[]{:S(2)}, u32[]{:S(2)}) collective-permute-start(bf16[2,4,256,128]{3,2,1,0:T(8,128)(2,1)S(1)} %pad_maximum_fusion.6.refs_1_), channel_id=1, source_target_pairs={{0,192},{64,0},{128,64},{192,128},{1,193},{65,1},{129,65},{193,129... | collective-permute-start | bytes 1572872 | tf_op jit(solution)/shard_map/ppermute | solution.py:25
  95.3 3.1 %collective-permute-start.13 = (bf16[256,128]{1,0:T(8,128)(2,1)S(1)}, bf16[256,128]{1,0:T(8,128)(2,1)S(1)}, u32[]{:S(2)}, u32[]{:S(2)}) collective-permute-start(bf16[256,128]{1,0:T(8,128)(2,1)S(1)} %get-tuple-element.28), channel_id=1, source_target_pairs={{0,16},{16,32},{32,48},{48,0},{1,17},{17,33},{33,49},{49,1},{2,18}... | collective-permute-start | bytes 196616 | tf_op jit(solution)/shard_map/ppermute | solution.py:25
  98.9 1.7 collective-permute-start.15
  100.5 4.0 %collective-permute-done.21.refs_2_ = bf16[2,4,256,128]{3,2,1,0:T(8,128)(2,1)S(1)} collective-permute-done((bf16[2,4,256,128]{3,2,1,0:T(8,128)(2,1)S(1)}, bf16[2,4,256,128]{3,2,1,0:T(8,128)(2,1)S(1)}, u32[]{:S(2)}, u32[]{:S(2)}) %collective-permute-start.21) | collective-permute-done | bytes 524320 | tf_op jit(solution)/shard_map/ppermute | solution.py:25
  104.5 2.9 %collective-permute-start.25 = (bf16[2,4,256,128]{3,2,1,0:T(8,128)(2,1)S(1)}, bf16[2,4,256,128]{3,2,1,0:T(8,128)(2,1)S(1)}, u32[]{:S(2)}, u32[]{:S(2)}) collective-permute-start(bf16[2,4,256,128]{3,2,1,0:T(8,128)(2,1)S(1)} %pad_maximum_fusion.6.refs_1_), channel_id=1, source_target_pairs={{0,8},{8,0},{1,9},{9,1},{2,10},{10,2},{3,11},{11,3},{4,12},{12,4},... | collective-permute-start | bytes 1572872 | tf_op jit(solution)/shard_map/ppermute | solution.py:25
  107.7 3.3 %collective-permute-start.24 = (bf16[2,2,4,256,128]{4,3,2,1,0:T(8,128)(2,1)S(1)}, bf16[2,2,4,256,128]{4,3,2,1,0:T(8,128)(2,1)S(1)}, u32[]{:S(2)}, u32[]{:S(2)}) collective-permute-start(bf16[2,2,4,256,128]{4,3,2,1,0:T(8,128)(2,1)S(1)} %pad_maximum_fusion), channel_id=1, source_target_pairs={{0,8},{8,0},{1,9},{9,1},{2,10},{10,2},{3,11},{11,3},{4,12},{12,4},... | collective-permute-start | bytes 3145736 | tf_op jit(solution)/shard_map/ppermute | solution.py:25
  111.2 1.4 collective-permute-start.20
  113.2 5.8 %collective-permute-done.22.refs_2_ = bf16[4,256,128]{2,1,0:T(8,128)(2,1)S(1)} collective-permute-done((bf16[4,256,128]{2,1,0:T(8,128)(2,1)S(1)}, bf16[4,256,128]{2,1,0:T(8,128)(2,1)S(1)}, u32[]{:S(2)}, u32[]{:S(2)}) %collective-permute-start.22) | collective-permute-done | bytes 262176 | tf_op jit(solution)/shard_map/ppermute | solution.py:25
  119.7 1.9 collective-permute-start.23
  121.5 4.2 %shard_map.57 = (f32[4,256,128]{2,1,0:T(8,128)S(1)}, f32[4,256,128]{2,1,0:T(8,128)S(1)}, f32[4,256,128]{2,1,0:T(8,128)S(1)}) custom-call(bf16[4,256,128]{2,1,0:T(8,128)(2,1)S(1)} %pad_maximum_fusion.8.refs_0_, bf16[2,4,256,128]{3,2,1,0:T(8,128)(2,1)S(1)} %pad_maximum_fusion.6.refs_1_, bf16[2,4,256,128]{3,2,1,0:T(8,128)(2,1)S(1)} %collective-permute-done.25.refs_2_), custom_call_target="tpu_custom_call" | custom-call | flops 2147483648 | bytes 1048576 | tf_op jit(solution)/shard_map/pallas_call | solution.py:42
  125.8 5.1 %shard_map.58 = (f32[4,256,128]{2,1,0:T(8,128)S(1)}, f32[4,256,128]{2,1,0:T(8,128)S(1)}, f32[4,256,128]{2,1,0:T(8,128)S(1)}) custom-call(bf16[4,256,128]{2,1,0:T(8,128)(2,1)S(1)} %pad_maximum_fusion.8.refs_0_, bf16[2,4,256,128]{3,2,1,0:T(8,128)(2,1)S(1)} %collective-permute-done.19.refs_1_, bf16[2,4,256,128]{3,2,1,0:T(8,128)(2,1)S(1)} %collective-permute-done.21.refs_2_, ...), custom_call_target="tpu_custom_call" | custom-call | flops 2147483648 | bytes 1048576 | tf_op jit(solution)/shard_map/pallas_call | solution.py:42
  130.8 5.1 %shard_map.59 = (f32[4,256,128]{2,1,0:T(8,128)S(1)}, f32[4,256,128]{2,1,0:T(8,128)S(1)}, f32[4,256,128]{2,1,0:T(8,128)S(1)}) custom-call(bf16[4,256,128]{2,1,0:T(8,128)(2,1)S(1)} %pad_maximum_fusion.8.refs_0_, bf16[2,2,4,256,128]{4,3,2,1,0:T(8,128)(2,1)S(1)} %collective-permute-done.24.refs_1_, f32[4,256,128]{2,1,0:T(8,128)S(1)} %get-tuple-element.38.refs_2_, ...), custom_call_target="tpu_custom_call" | custom-call | flops 2147483648 | bytes 1048576 | tf_op jit(solution)/shard_map/pallas_call | solution.py:42
  135.9 5.0 %shard_map.60 = bf16[4,256,128]{2,1,0:T(8,128)(2,1)S(1)} custom-call(bf16[4,256,128]{2,1,0:T(8,128)(2,1)S(1)} %pad_maximum_fusion.8.refs_0_, bf16[4,256,128]{2,1,0:T(8,128)(2,1)S(1)} %collective-permute-done.20.refs_1_, bf16[4,256,128]{2,1,0:T(8,128)(2,1)S(1)} %collective-permute-done.22.refs_2_, ...), custom_call_target="tpu_custom_call" | custom-call | flops 2147483648 | bytes 1048576 | tf_op jit(solution)/shard_map/pallas_call | solution.py:42
  141.0 3.2 %collective-permute-start.28 = (bf16[256,128]{1,0:T(8,128)(2,1)S(1)}, bf16[256,128]{1,0:T(8,128)(2,1)S(1)}, u32[]{:S(2)}, u32[]{:S(2)}) collective-permute-start(bf16[256,128]{1,0:T(8,128)(2,1)S(1)} %get-tuple-element.53), channel_id=1, source_target_pairs={{0,16},{16,32},{32,48},{48,0},{1,17},{17,33},{33,49},{49,1},{2,18}... | collective-permute-start | bytes 196616 | tf_op jit(solution)/shard_map/ppermute | solution.py:25
  144.7 1.7 collective-permute-start.26
  146.6 3.7 %collective-permute-done.27.c2 = bf16[256,128]{1,0:T(8,128)(2,1)S(1)} collective-permute-done((bf16[256,128]{1,0:T(8,128)(2,1)S(1)}, bf16[256,128]{1,0:T(8,128)(2,1)S(1)}, u32[]{:S(2)}, u32[]{:S(2)}) %collective-permute-start.27) | collective-permute-done | bytes 65568 | tf_op jit(solution)/shard_map/ppermute | solution.py:25
  150.5 1.2 collective-permute-start.30
  152.1 3.0 %collective-permute-start.35 = (bf16[2,512,384]{2,1,0:T(8,128)(2,1)S(1)}, bf16[2,512,384]{2,1,0:T(8,128)(2,1)S(1)}, u32[]{:S(2)}, u32[]{:S(2)}) collective-permute-start(bf16[2,512,384]{2,1,0:T(8,128)(2,1)S(1)} %pad_maximum_fusion.4), channel_id=1, source_target_pairs={{0,2},{1,3},{2,0},{3,1},{4,6},{5,7},{6,4},{7,5},{8,10},{9,11},{10,... | collective-permute-start | bytes 2359304 | tf_op jit(solution)/shard_map/ppermute | solution.py:25
  155.2 16.0 %collective-permute-done.31 = bf16[256,512]{1,0:T(8,128)(2,1)S(1)} collective-permute-done((bf16[256,512]{1,0:T(8,128)(2,1)S(1)}, bf16[256,512]{1,0:T(8,128)(2,1)S(1)}, u32[]{:S(2)}, u32[]{:S(2)}) %collective-permute-start.31) | collective-permute-done | bytes 262176 | tf_op jit(solution)/shard_map/ppermute | solution.py:25
  171.2 6.9 %collective-permute-done.29 = bf16[256,512]{1,0:T(8,128)(2,1)S(1)} collective-permute-done((bf16[256,512]{1,0:T(8,128)(2,1)S(1)}, bf16[256,512]{1,0:T(8,128)(2,1)S(1)}, u32[]{:S(2)}, u32[]{:S(2)}) %collective-permute-start.29) | collective-permute-done | bytes 262176 | tf_op jit(solution)/shard_map/ppermute | solution.py:25
  178.2 17.8 %collective-permute-start.33 = (bf16[3,256,512]{2,1,0:T(8,128)(2,1)S(1)}, bf16[3,256,512]{2,1,0:T(8,128)(2,1)S(1)}, u32[]{:S(2)}, u32[]{:S(2)}) collective-permute-start(bf16[3,256,512]{2,1,0:T(8,128)(2,1)S(1)} %pad_maximum_fusion.1.rest), channel_id=1, source_target_pairs={{0,8},{8,0},{1,9},{9,1},{2,10},{10,2},{3,11},{11,3},{4,12},{12,4},... | collective-permute-start | bytes 2359304 | tf_op jit(solution)/shard_map/ppermute | solution.py:25
  197.9 2.0 collective-permute-start.37
  200.6 3.6 %collective-permute-start.38 = (bf16[256,384]{1,0:T(8,128)(2,1)S(1)}, bf16[256,384]{1,0:T(8,128)(2,1)S(1)}, u32[]{:S(2)}, u32[]{:S(2)}) collective-permute-start(bf16[256,384]{1,0:T(8,128)(2,1)S(1)} %shard_map.64), channel_id=1, source_target_pairs={{0,4},{4,0},{1,5},{5,1},{2,6},{6,2},{3,7},{7,3},{8,12},{12,8},{9,1... | collective-permute-start | bytes 589832 | tf_op jit(solution)/shard_map/ppermute | solution.py:25
  204.1 1.2 shard_map.62.own
  205.4 7.7 %collective-permute-done.37.first = bf16[256,384]{1,0:T(8,128)(2,1)S(1)} collective-permute-done((bf16[256,384]{1,0:T(8,128)(2,1)S(1)}, bf16[256,384]{1,0:T(8,128)(2,1)S(1)}, u32[]{:S(2)}, u32[]{:S(2)}) %collective-permute-start.37) | collective-permute-done | bytes 196640 | tf_op jit(solution)/shard_map/ppermute | solution.py:25
  213.1 8.0 %collective-permute-done.38.second = bf16[256,384]{1,0:T(8,128)(2,1)S(1)} collective-permute-done((bf16[256,384]{1,0:T(8,128)(2,1)S(1)}, bf16[256,384]{1,0:T(8,128)(2,1)S(1)}, u32[]{:S(2)}, u32[]{:S(2)}) %collective-permute-start.38) | collective-permute-done | bytes 196640 | tf_op jit(solution)/shard_map/ppermute | solution.py:25
  (78 shorter events, 13.9 us)
Async XLA Ops:
  0.0 34.8 %collective-permute-start.5 = (bf16[512,384]{1,0:T(8,128)(2,1)}, bf16[512,384]{1,0:T(8,128)(2,1)S(1)}, u32[]{:S(2)}, u32[]{:S(2)}) collective-permute-start(bf16[512,384]{1,0:T(8,128)(2,1)} %tokens.3), channel_id=1, source_target_pairs={{0,4},{4,0},{1,5},{5,1},{2,6},{6,2},{3,7},{7,3},{8,12},{12,8},{9,1... | collective-permute-start | bytes 1179656 | tf_op jit(solution)/shard_map/ppermute | solution.py:25
  7.7 29.8 %collective-permute-start.11 = (bf16[512,384]{1,0:T(8,128)(2,1)}, bf16[512,384]{1,0:T(8,128)(2,1)}, u32[]{:S(2)}, u32[]{:S(2)}) collective-permute-start(bf16[512,384]{1,0:T(8,128)(2,1)} %tokens.3), channel_id=1, source_target_pairs={{0,2},{1,3},{2,0},{3,1},{4,6},{5,7},{6,4},{7,5},{8,10},{9,11},{10,... | collective-permute-start | bytes 1179656 | tf_op jit(solution)/shard_map/ppermute | solution.py:25
  12.0 1.0 copy-start
  13.4 6.1 %collective-permute-start.2 = (f32[4,512]{1,0:T(4,128)S(1)}, f32[4,512]{1,0:T(4,128)S(1)}, u32[]{:S(2)}, u32[]{:S(2)}) collective-permute-start(f32[4,512]{1,0:T(4,128)S(1)} %shard_map.55), channel_id=1, source_target_pairs={{0,2},{1,3},{2,0},{3,1},{4,6},{5,7},{6,4},{7,5},{8,10},{9,11},{10,... | collective-permute-start | bytes 24584 | tf_op jit(solution)/shard_map/ppermute | solution.py:25
  13.5 6.5 %collective-permute-start.1 = (f32[4,512]{1,0:T(4,128)S(1)}, f32[4,512]{1,0:T(4,128)S(1)}, u32[]{:S(2)}, u32[]{:S(2)}) collective-permute-start(f32[4,512]{1,0:T(4,128)S(1)} %shard_map.55), channel_id=1, source_target_pairs={{0,3},{1,0},{2,1},{3,2},{4,7},{5,4},{6,5},{7,6},{8,11},{9,8},{10,9... | collective-permute-start | bytes 24584 | tf_op jit(solution)/shard_map/ppermute | solution.py:25
  16.2 4.7 %collective-permute-start = (f32[4,512]{1,0:T(4,128)S(1)}, f32[4,512]{1,0:T(4,128)S(1)}, u32[]{:S(2)}, u32[]{:S(2)}) collective-permute-start(f32[4,512]{1,0:T(4,128)S(1)} %shard_map.55), channel_id=1, source_target_pairs={{0,1},{1,2},{2,3},{3,0},{4,5},{5,6},{6,7},{7,4},{8,9},{9,10},{10,1... | collective-permute-start | bytes 24584 | tf_op jit(solution)/shard_map/ppermute | solution.py:25
  20.9 10.2 %collective-permute-start.3 = (f32[4,4,512]{2,1,0:T(4,128)S(1)}, f32[4,4,512]{2,1,0:T(4,128)S(1)}, u32[]{:S(2)}, u32[]{:S(2)}) collective-permute-start(f32[4,4,512]{2,1,0:T(4,128)S(1)} %pad_maximum_fusion.9.facts), channel_id=1, source_target_pairs={{0,4},{4,0},{1,5},{5,1},{2,6},{6,2},{3,7},{7,3},{8,12},{12,8},{9,1... | collective-permute-start | bytes 98312 | tf_op jit(solution)/shard_map/ppermute | solution.py:25
  31.1 5.3 %collective-permute-start.4 = (f32[2,512]{1,0:T(2,128)S(1)}, f32[2,512]{1,0:T(2,128)S(1)}, u32[]{:S(2)}, u32[]{:S(2)}) collective-permute-start(f32[2,512]{1,0:T(2,128)S(1)} %fusion), channel_id=1, source_target_pairs={{0,8},{8,0},{1,9},{9,1},{2,10},{10,2},{3,11},{11,3},{4,12},{12,4},... | collective-permute-start | bytes 12296 | tf_op jit(solution)/shard_map/ppermute | solution.py:25
  31.7 20.1 %collective-permute-start.10 = (bf16[512,384]{1,0:T(8,128)(2,1)}, bf16[512,384]{1,0:T(8,128)(2,1)S(1)}, u32[]{:S(2)}, u32[]{:S(2)}) collective-permute-start(bf16[512,384]{1,0:T(8,128)(2,1)} %tokens.3), channel_id=1, source_target_pairs={{0,3},{1,0},{2,1},{3,2},{4,7},{5,4},{6,5},{7,6},{8,11},{9,8},{10,9... | collective-permute-start | bytes 1179656 | tf_op jit(solution)/shard_map/ppermute | solution.py:25
  34.8 19.5 %collective-permute-start.9 = (bf16[512,384]{1,0:T(8,128)(2,1)}, bf16[512,384]{1,0:T(8,128)(2,1)S(1)}, u32[]{:S(2)}, u32[]{:S(2)}) collective-permute-start(bf16[512,384]{1,0:T(8,128)(2,1)} %tokens.3), channel_id=1, source_target_pairs={{0,1},{1,2},{2,3},{3,0},{4,5},{5,6},{6,7},{7,4},{8,9},{9,10},{10,1... | collective-permute-start | bytes 1179656 | tf_op jit(solution)/shard_map/ppermute | solution.py:25
  34.8 19.5 %collective-permute-start.8 = (bf16[512,384]{1,0:T(8,128)(2,1)S(1)}, bf16[512,384]{1,0:T(8,128)(2,1)S(1)}, u32[]{:S(2)}, u32[]{:S(2)}) collective-permute-start(bf16[512,384]{1,0:T(8,128)(2,1)S(1)} %collective-permute-done.5.refs_0_), channel_id=1, source_target_pairs={{0,2},{1,3},{2,0},{3,1},{4,6},{5,7},{6,4},{7,5},{8,10},{9,11},{10,... | collective-permute-start | bytes 1179656 | tf_op jit(solution)/shard_map/ppermute | solution.py:25
  36.4 23.8 %collective-permute-start.7 = (bf16[512,384]{1,0:T(8,128)(2,1)S(1)}, bf16[512,384]{1,0:T(8,128)(2,1)S(1)}, u32[]{:S(2)}, u32[]{:S(2)}) collective-permute-start(bf16[512,384]{1,0:T(8,128)(2,1)S(1)} %collective-permute-done.5.refs_0_), channel_id=1, source_target_pairs={{0,3},{1,0},{2,1},{3,2},{4,7},{5,4},{6,5},{7,6},{8,11},{9,8},{10,9... | collective-permute-start | bytes 1179656 | tf_op jit(solution)/shard_map/ppermute | solution.py:25
  37.5 25.8 %collective-permute-start.6 = (bf16[512,384]{1,0:T(8,128)(2,1)S(1)}, bf16[512,384]{1,0:T(8,128)(2,1)S(1)}, u32[]{:S(2)}, u32[]{:S(2)}) collective-permute-start(bf16[512,384]{1,0:T(8,128)(2,1)S(1)} %collective-permute-done.5.refs_0_), channel_id=1, source_target_pairs={{0,1},{1,2},{2,3},{3,0},{4,5},{5,6},{6,7},{7,4},{8,9},{9,10},{10,1... | collective-permute-start | bytes 1179656 | tf_op jit(solution)/shard_map/ppermute | solution.py:25
  51.7 8.5 %copy-start.7 = (bf16[512,384]{1,0:T(8,128)(2,1)}, bf16[512,384]{1,0:T(8,128)(2,1)S(1)}, u32[]{:S(2)}) copy-start(bf16[512,384]{1,0:T(8,128)(2,1)S(1)} %collective-permute-done.10.refs_6_) | copy-start | bytes 1179652
  54.2 6.0 %copy-start.8 = (bf16[512,384]{1,0:T(8,128)(2,1)}, bf16[512,384]{1,0:T(8,128)(2,1)S(1)}, u32[]{:S(2)}) copy-start(bf16[512,384]{1,0:T(8,128)(2,1)S(1)} %collective-permute-done.9.refs_5_) | copy-start | bytes 1179652
  60.2 0.8 copy-start.2
  63.3 0.7 copy-start.4
  64.1 1.0 copy-start.3
  65.1 1.0 copy-start.5
  77.6 3.2 %collective-permute-start.12 = (bf16[256,1536]{1,0:T(8,128)(2,1)S(1)}, bf16[256,1536]{1,0:T(8,128)(2,1)S(1)}, u32[]{:S(2)}, u32[]{:S(2)}) collective-permute-start(bf16[256,1536]{1,0:T(8,128)(2,1)S(1)} %get-tuple-element.26), channel_id=1, source_target_pairs={{0,8},{8,0},{1,9},{9,1},{2,10},{10,2},{3,11},{11,3},{4,12},{12,4},... | collective-permute-start | bytes 2359304 | tf_op jit(solution)/shard_map/ppermute | solution.py:25
  81.2 6.6 %collective-permute-start.16 = (bf16[2,256,128]{2,1,0:T(8,128)(2,1)S(1)}, bf16[2,256,128]{2,1,0:T(8,128)(2,1)S(1)}, u32[]{:S(2)}, u32[]{:S(2)}) collective-permute-start(bf16[2,256,128]{2,1,0:T(8,128)(2,1)S(1)} %get-tuple-element.32), channel_id=1, source_target_pairs={{0,16},{16,32},{32,48},{48,0},{1,17},{17,33},{33,49},{49,1},{2,18}... | collective-permute-start | bytes 393224 | tf_op jit(solution)/shard_map/ppermute | solution.py:25
  81.3 11.3 %collective-permute-start.17 = (bf16[2,256,128]{2,1,0:T(8,128)(2,1)S(1)}, bf16[2,256,128]{2,1,0:T(8,128)(2,1)S(1)}, u32[]{:S(2)}, u32[]{:S(2)}) collective-permute-start(bf16[2,256,128]{2,1,0:T(8,128)(2,1)S(1)} %get-tuple-element.33), channel_id=1, source_target_pairs={{0,32},{16,48},{32,0},{48,16},{1,33},{17,49},{33,1},{49,17},{2,34}... | collective-permute-start | bytes 393224 | tf_op jit(solution)/shard_map/ppermute | solution.py:25
  82.5 10.1 %collective-permute-start.18 = (bf16[2,256,128]{2,1,0:T(8,128)(2,1)S(1)}, bf16[2,256,128]{2,1,0:T(8,128)(2,1)S(1)}, u32[]{:S(2)}, u32[]{:S(2)}) collective-permute-start(bf16[2,256,128]{2,1,0:T(8,128)(2,1)S(1)} %get-tuple-element.34), channel_id=1, source_target_pairs={{0,48},{16,0},{32,16},{48,32},{1,49},{17,1},{33,17},{49,33},{2,50}... | collective-permute-start | bytes 393224 | tf_op jit(solution)/shard_map/ppermute | solution.py:25
  92.7 11.8 %collective-permute-start.21 = (bf16[2,4,256,128]{3,2,1,0:T(8,128)(2,1)S(1)}, bf16[2,4,256,128]{3,2,1,0:T(8,128)(2,1)S(1)}, u32[]{:S(2)}, u32[]{:S(2)}) collective-permute-start(bf16[2,4,256,128]{3,2,1,0:T(8,128)(2,1)S(1)} %pad_maximum_fusion.6.refs_1_), channel_id=1, source_target_pairs={{0,192},{64,0},{128,64},{192,128},{1,193},{65,1},{129,65},{193,129... | collective-permute-start | bytes 1572872 | tf_op jit(solution)/shard_map/ppermute | solution.py:25
  95.3 12.4 %collective-permute-start.19 = (bf16[2,4,256,128]{3,2,1,0:T(8,128)(2,1)S(1)}, bf16[2,4,256,128]{3,2,1,0:T(8,128)(2,1)S(1)}, u32[]{:S(2)}, u32[]{:S(2)}) collective-permute-start(bf16[2,4,256,128]{3,2,1,0:T(8,128)(2,1)S(1)} %pad_maximum_fusion.6.refs_1_), channel_id=1, source_target_pairs={{0,64},{64,128},{128,192},{192,0},{1,65},{65,129},{129,193},{193,1... | collective-permute-start | bytes 1572872 | tf_op jit(solution)/shard_map/ppermute | solution.py:25
  95.3 17.3 %copy-start.6 = (bf16[512,3072]{1,0:T(8,128)(2,1)S(1)}, bf16[512,3072]{1,0:T(8,128)(2,1)}, u32[]{:S(2)}) copy-start(bf16[512,3072]{1,0:T(8,128)(2,1)} %param.9) | copy-start | bytes 9437188
  95.3 15.8 %collective-permute-start.13 = (bf16[256,128]{1,0:T(8,128)(2,1)S(1)}, bf16[256,128]{1,0:T(8,128)(2,1)S(1)}, u32[]{:S(2)}, u32[]{:S(2)}) collective-permute-start(bf16[256,128]{1,0:T(8,128)(2,1)S(1)} %get-tuple-element.28), channel_id=1, source_target_pairs={{0,16},{16,32},{32,48},{48,0},{1,17},{17,33},{33,49},{49,1},{2,18}... | collective-permute-start | bytes 196616 | tf_op jit(solution)/shard_map/ppermute | solution.py:25
  98.4 12.8 %collective-permute-start.14 = (bf16[256,128]{1,0:T(8,128)(2,1)S(1)}, bf16[256,128]{1,0:T(8,128)(2,1)S(1)}, u32[]{:S(2)}, u32[]{:S(2)}) collective-permute-start(bf16[256,128]{1,0:T(8,128)(2,1)S(1)} %get-tuple-element.29), channel_id=1, source_target_pairs={{0,32},{16,48},{32,0},{48,16},{1,33},{17,49},{33,1},{49,17},{2,34}... | collective-permute-start | bytes 196616 | tf_op jit(solution)/shard_map/ppermute | solution.py:25
  98.9 14.3 %collective-permute-start.15 = (bf16[256,128]{1,0:T(8,128)(2,1)S(1)}, bf16[256,128]{1,0:T(8,128)(2,1)S(1)}, u32[]{:S(2)}, u32[]{:S(2)}) collective-permute-start(bf16[256,128]{1,0:T(8,128)(2,1)S(1)} %get-tuple-element.30), channel_id=1, source_target_pairs={{0,48},{16,0},{32,16},{48,32},{1,49},{17,1},{33,17},{49,33},{2,50}... | collective-permute-start | bytes 196616 | tf_op jit(solution)/shard_map/ppermute | solution.py:25
  104.5 17.0 %collective-permute-start.25 = (bf16[2,4,256,128]{3,2,1,0:T(8,128)(2,1)S(1)}, bf16[2,4,256,128]{3,2,1,0:T(8,128)(2,1)S(1)}, u32[]{:S(2)}, u32[]{:S(2)}) collective-permute-start(bf16[2,4,256,128]{3,2,1,0:T(8,128)(2,1)S(1)} %pad_maximum_fusion.6.refs_1_), channel_id=1, source_target_pairs={{0,8},{8,0},{1,9},{9,1},{2,10},{10,2},{3,11},{11,3},{4,12},{12,4},... | collective-permute-start | bytes 1572872 | tf_op jit(solution)/shard_map/ppermute | solution.py:25
  107.7 23.1 %collective-permute-start.24 = (bf16[2,2,4,256,128]{4,3,2,1,0:T(8,128)(2,1)S(1)}, bf16[2,2,4,256,128]{4,3,2,1,0:T(8,128)(2,1)S(1)}, u32[]{:S(2)}, u32[]{:S(2)}) collective-permute-start(bf16[2,2,4,256,128]{4,3,2,1,0:T(8,128)(2,1)S(1)} %pad_maximum_fusion), channel_id=1, source_target_pairs={{0,8},{8,0},{1,9},{9,1},{2,10},{10,2},{3,11},{11,3},{4,12},{12,4},... | collective-permute-start | bytes 3145736 | tf_op jit(solution)/shard_map/ppermute | solution.py:25
  111.1 7.9 %collective-permute-start.22 = (bf16[4,256,128]{2,1,0:T(8,128)(2,1)S(1)}, bf16[4,256,128]{2,1,0:T(8,128)(2,1)S(1)}, u32[]{:S(2)}, u32[]{:S(2)}) collective-permute-start(bf16[4,256,128]{2,1,0:T(8,128)(2,1)S(1)} %slice_bitcast_fusion), channel_id=1, source_target_pairs={{0,192},{64,0},{128,64},{192,128},{1,193},{65,1},{129,65},{193,129... | collective-permute-start | bytes 786440 | tf_op jit(solution)/shard_map/ppermute | solution.py:25
  111.2 8.5 %collective-permute-start.20 = (bf16[4,256,128]{2,1,0:T(8,128)(2,1)S(1)}, bf16[4,256,128]{2,1,0:T(8,128)(2,1)S(1)}, u32[]{:S(2)}, u32[]{:S(2)}) collective-permute-start(bf16[4,256,128]{2,1,0:T(8,128)(2,1)S(1)} %slice_bitcast_fusion.1), channel_id=1, source_target_pairs={{0,64},{64,128},{128,192},{192,0},{1,65},{65,129},{129,193},{193,1... | collective-permute-start | bytes 786440 | tf_op jit(solution)/shard_map/ppermute | solution.py:25
  119.7 16.2 %collective-permute-start.23 = (bf16[2,4,256,128]{3,2,1,0:T(8,128)(2,1)S(1)}, bf16[2,4,256,128]{3,2,1,0:T(8,128)(2,1)S(1)}, u32[]{:S(2)}, u32[]{:S(2)}) collective-permute-start(bf16[2,4,256,128]{3,2,1,0:T(8,128)(2,1)S(1)} %pad_maximum_fusion.7), channel_id=1, source_target_pairs={{0,8},{8,0},{1,9},{9,1},{2,10},{10,2},{3,11},{11,3},{4,12},{12,4},... | collective-permute-start | bytes 1572872 | tf_op jit(solution)/shard_map/ppermute | solution.py:25
  141.0 5.6 %collective-permute-start.28 = (bf16[256,128]{1,0:T(8,128)(2,1)S(1)}, bf16[256,128]{1,0:T(8,128)(2,1)S(1)}, u32[]{:S(2)}, u32[]{:S(2)}) collective-permute-start(bf16[256,128]{1,0:T(8,128)(2,1)S(1)} %get-tuple-element.53), channel_id=1, source_target_pairs={{0,16},{16,32},{32,48},{48,0},{1,17},{17,33},{33,49},{49,1},{2,18}... | collective-permute-start | bytes 196616 | tf_op jit(solution)/shard_map/ppermute | solution.py:25
  144.1 6.2 %collective-permute-start.27 = (bf16[256,128]{1,0:T(8,128)(2,1)S(1)}, bf16[256,128]{1,0:T(8,128)(2,1)S(1)}, u32[]{:S(2)}, u32[]{:S(2)}) collective-permute-start(bf16[256,128]{1,0:T(8,128)(2,1)S(1)} %get-tuple-element.54), channel_id=1, source_target_pairs={{0,32},{16,48},{32,0},{48,16},{1,33},{17,49},{33,1},{49,17},{2,34}... | collective-permute-start | bytes 196616 | tf_op jit(solution)/shard_map/ppermute | solution.py:25
  144.7 5.7 %collective-permute-start.26 = (bf16[256,128]{1,0:T(8,128)(2,1)S(1)}, bf16[256,128]{1,0:T(8,128)(2,1)S(1)}, u32[]{:S(2)}, u32[]{:S(2)}) collective-permute-start(bf16[256,128]{1,0:T(8,128)(2,1)S(1)} %get-tuple-element.55), channel_id=1, source_target_pairs={{0,48},{16,0},{32,16},{48,32},{1,49},{17,1},{33,17},{49,33},{2,50}... | collective-permute-start | bytes 196616 | tf_op jit(solution)/shard_map/ppermute | solution.py:25
  146.4 50.0 %collective-permute-start.34 = (bf16[2,512,384]{2,1,0:T(8,128)(2,1)S(1)}, bf16[2,512,384]{2,1,0:T(8,128)(2,1)S(1)}, u32[]{:S(2)}, u32[]{:S(2)}) collective-permute-start(bf16[2,512,384]{2,1,0:T(8,128)(2,1)S(1)} %pad_maximum_fusion.3), channel_id=1, source_target_pairs={{0,1},{1,2},{2,3},{3,0},{4,5},{5,6},{6,7},{7,4},{8,9},{9,10},{10,1... | collective-permute-start | bytes 2359304 | tf_op jit(solution)/shard_map/ppermute | solution.py:25
  150.4 20.8 %collective-permute-start.31 = (bf16[256,512]{1,0:T(8,128)(2,1)S(1)}, bf16[256,512]{1,0:T(8,128)(2,1)S(1)}, u32[]{:S(2)}, u32[]{:S(2)}) collective-permute-start(bf16[256,512]{1,0:T(8,128)(2,1)S(1)} %shard_map.61.own), channel_id=1, source_target_pairs={{0,2},{1,3},{2,0},{3,1},{4,6},{5,7},{6,4},{7,5},{8,10},{9,11},{10,... | collective-permute-start | bytes 786440 | tf_op jit(solution)/shard_map/ppermute | solution.py:25
  150.5 20.7 %collective-permute-start.30 = (bf16[256,512]{1,0:T(8,128)(2,1)S(1)}, bf16[256,512]{1,0:T(8,128)(2,1)S(1)}, u32[]{:S(2)}, u32[]{:S(2)}) collective-permute-start(bf16[256,512]{1,0:T(8,128)(2,1)S(1)} %shard_map.61.own), channel_id=1, source_target_pairs={{0,3},{1,0},{2,1},{3,2},{4,7},{5,4},{6,5},{7,6},{8,11},{9,8},{10,9... | collective-permute-start | bytes 786440 | tf_op jit(solution)/shard_map/ppermute | solution.py:25
  151.8 26.3 %collective-permute-start.29 = (bf16[256,512]{1,0:T(8,128)(2,1)S(1)}, bf16[256,512]{1,0:T(8,128)(2,1)S(1)}, u32[]{:S(2)}, u32[]{:S(2)}) collective-permute-start(bf16[256,512]{1,0:T(8,128)(2,1)S(1)} %shard_map.61.own), channel_id=1, source_target_pairs={{0,1},{1,2},{2,3},{3,0},{4,5},{5,6},{6,7},{7,4},{8,9},{9,10},{10,1... | collective-permute-start | bytes 786440 | tf_op jit(solution)/shard_map/ppermute | solution.py:25
  152.1 44.3 %collective-permute-start.35 = (bf16[2,512,384]{2,1,0:T(8,128)(2,1)S(1)}, bf16[2,512,384]{2,1,0:T(8,128)(2,1)S(1)}, u32[]{:S(2)}, u32[]{:S(2)}) collective-permute-start(bf16[2,512,384]{2,1,0:T(8,128)(2,1)S(1)} %pad_maximum_fusion.4), channel_id=1, source_target_pairs={{0,2},{1,3},{2,0},{3,1},{4,6},{5,7},{6,4},{7,5},{8,10},{9,11},{10,... | collective-permute-start | bytes 2359304 | tf_op jit(solution)/shard_map/ppermute | solution.py:25
  171.2 25.9 %collective-permute-start.36 = (bf16[2,512,384]{2,1,0:T(8,128)(2,1)S(1)}, bf16[2,512,384]{2,1,0:T(8,128)(2,1)S(1)}, u32[]{:S(2)}, u32[]{:S(2)}) collective-permute-start(bf16[2,512,384]{2,1,0:T(8,128)(2,1)S(1)} %pad_maximum_fusion.5), channel_id=1, source_target_pairs={{0,3},{1,0},{2,1},{3,2},{4,7},{5,4},{6,5},{7,6},{8,11},{9,8},{10,9... | collective-permute-start | bytes 2359304 | tf_op jit(solution)/shard_map/ppermute | solution.py:25
  178.2 21.7 %collective-permute-start.33 = (bf16[3,256,512]{2,1,0:T(8,128)(2,1)S(1)}, bf16[3,256,512]{2,1,0:T(8,128)(2,1)S(1)}, u32[]{:S(2)}, u32[]{:S(2)}) collective-permute-start(bf16[3,256,512]{2,1,0:T(8,128)(2,1)S(1)} %pad_maximum_fusion.1.rest), channel_id=1, source_target_pairs={{0,8},{8,0},{1,9},{9,1},{2,10},{10,2},{3,11},{11,3},{4,12},{12,4},... | collective-permute-start | bytes 2359304 | tf_op jit(solution)/shard_map/ppermute | solution.py:25
  195.9 3.9 %collective-permute-start.32 = (bf16[256,512]{1,0:T(8,128)(2,1)S(1)}, bf16[256,512]{1,0:T(8,128)(2,1)S(1)}, u32[]{:S(2)}, u32[]{:S(2)}) collective-permute-start(bf16[256,512]{1,0:T(8,128)(2,1)S(1)} %shard_map.61.own), channel_id=1, source_target_pairs={{0,8},{8,0},{1,9},{9,1},{2,10},{10,2},{3,11},{11,3},{4,12},{12,4},... | collective-permute-start | bytes 786440 | tf_op jit(solution)/shard_map/ppermute | solution.py:25
  197.9 15.2 %collective-permute-start.37 = (bf16[256,384]{1,0:T(8,128)(2,1)S(1)}, bf16[256,384]{1,0:T(8,128)(2,1)S(1)}, u32[]{:S(2)}, u32[]{:S(2)}) collective-permute-start(bf16[256,384]{1,0:T(8,128)(2,1)S(1)} %shard_map.63), channel_id=1, source_target_pairs={{0,4},{4,0},{1,5},{5,1},{2,6},{6,2},{3,7},{7,3},{8,12},{12,8},{9,1... | collective-permute-start | bytes 589832 | tf_op jit(solution)/shard_map/ppermute | solution.py:25
  200.6 20.6 %copy-start.1 = (bf16[512,384]{1,0:T(8,128)(2,1)S(1)}, bf16[512,384]{1,0:T(8,128)(2,1)}, u32[]{:S(2)}) copy-start(bf16[512,384]{1,0:T(8,128)(2,1)} %tokens.3) | copy-start | bytes 1179652
  200.6 20.6 %collective-permute-start.38 = (bf16[256,384]{1,0:T(8,128)(2,1)S(1)}, bf16[256,384]{1,0:T(8,128)(2,1)S(1)}, u32[]{:S(2)}, u32[]{:S(2)}) collective-permute-start(bf16[256,384]{1,0:T(8,128)(2,1)S(1)} %shard_map.64), channel_id=1, source_target_pairs={{0,4},{4,0},{1,5},{5,1},{2,6},{6,2},{3,7},{7,3},{8,12},{12,8},{9,1... | collective-permute-start | bytes 589832 | tf_op jit(solution)/shard_map/ppermute | solution.py:25
